TPU v7x, 32 devices: a whole 2x2x4 slice. The times are simulated.
32 devices in a mesh: gx: 4 (over y, core), gy: 8 (over z, x).
Axes of the slice: x: 2, y: 2, z: 4, core: 2. Of those that a mesh axis runs over, the one named last changes fastest.
Arguments:
- thermal_anomaly: float32 [32, 128, 1024], P(None, 'gx', 'gy'), may hold values from -6 to 6
- ambient_diffusion: bfloat16 [128, 1024], P('gx', 'gy'), may hold values from 0.019897461 to 0.25
- solar_light: bfloat16 [128, 1024], P('gx', 'gy'), may hold values from 0.5 to 4
- sea_tile_flags: int32 [4, 8, 64], P('gx', 'gy'), may hold values 0 or 1
- flooded_layer_tally: int32 [4, 8, 64], P('gx', 'gy'), may hold values from 1 to 32
- tile_holder_rank: int32 [4, 8, 64, 1], P('gx', 'gy'), may hold values from 0 to 7; in each aligned block of 64 rows (0 to 63, 64 to 127, ..., all dimensions but the last counted through in order) at most 16 rows name the same one
- solute_amounts: float32 [4, 8, 128, 8, 2048], P('gx', 'gy'), may hold values from 0.09 to 11
- reaction_rates: float32 [8, 8], replicated, may hold values from -0.2 to 0.5
Outputs:
- thermal_final: float32 [32, 128, 1024], P(None, 'gx', 'gy')
- solute_final: float32 [4, 8, 128, 8, 2048], P('gx', 'gy')
Inputs may be any that keep to these rules, and one draw needn't show every extreme that they name: `tile_holder_rank`: among the 64 blocks of one device, at most 16 name the same owner, a bound that some block reaches of them.
All inputs are finite; a program needn't handle non-finite values. No bound on the sum of `sea_tile_flags` on one device may be relied on, other than what follows from the above.
Results may differ from a plain program's by a relative error of at most 0.0003.
Values may be sent and summed in bfloat16 or wider, within the bound.
No kernel may reach another device: no remote copies, remote signals or barrier semaphores. Data moves between devices by JAX's collectives and lax.ppermute only.
A program may use at most 128 MiB of HBM per device.

v0:
```python
import jax
import jax.numpy as jnp
from jax import lax
from jax.sharding import PartitionSpec as P

NU_COEF = 0.2
STEP_DT = 0.05
ATTEN_WATER = 0.06
ATTEN_CHL = 0.05
WARMING_SCALE = 0.5
GROWTH_TEMP = 0.063


def with_halo(cells, sides, width):
    for axis, dim in sides:
        count = lax.axis_size(axis)
        ends = count - 1
        head = lax.slice_in_dim(cells, 0, width, axis=dim)
        tail = lax.slice_in_dim(cells, cells.shape[dim] - width, cells.shape[dim], axis=dim)
        cells = jnp.concatenate(
            [
                lax.ppermute(tail, axis, [(i, (i + 1) % count) for i in range(ends)]),
                cells,
                lax.ppermute(head, axis, [((i + 1) % count, i) for i in range(ends)]),
            ],
            axis=dim,
        )
    return cells


def masked_step(field, within_layer):
    center = field[:, 1:-1, 1:-1]
    span_east = center.shape[1]
    span_north = center.shape[2]
    total = jnp.zeros_like(center)
    for first, second in ((0, 1), (2, 1), (1, 0), (1, 2)):
        near = field[:, first : first + span_east, second : second + span_north]
        total = total + within_layer[:, first : first + span_east, second : second + span_north] * (
            near - center
        )
    return center + NU_COEF * within_layer[:, 1:-1, 1:-1] * total


def level_below(values):
    return jnp.concatenate([values[..., 64:], values[..., -64:]], axis=-1)


def level_above_zero(values):
    return jnp.concatenate([jnp.zeros_like(values[..., :64]), values[..., :-64]], axis=-1)


def level_prefix(values, layer_tally):
    running = values
    reach = 1
    while reach < layer_tally:
        moved = jnp.concatenate(
            [jnp.zeros_like(running[..., : 64 * reach]), running[..., : -64 * reach]], axis=-1
        )
        running = running + moved
        reach = reach * 2
    return running


def spread_levels(column_values, layer_tally):
    return jnp.tile(column_values, (1, layer_tally))


def flat_mixer(temp_flat, kbg_flat):
    return (kbg_flat * (1.0 + 0.5 * jnp.tanh(temp_flat - level_below(temp_flat)))).astype(
        jnp.bfloat16
    )


def flat_validity(tile_amount, flat_width):
    levels = lax.broadcasted_iota(jnp.int32, (1, flat_width), 1) // 64
    valid = (levels < tile_amount[:, None]).astype(jnp.float32)
    active = (levels + 1 < tile_amount[:, None]).astype(jnp.float32)
    return (valid, active)


def totals(amounts_on_chip, valid):
    return jnp.sum(amounts_on_chip * valid[:, None], axis=(0, 2))


def column_step(
    temp_flat, kappa_flat, surface, valid, active, amounts_on_chip, reaction_rates, layer_tally
):
    atten = ATTEN_WATER + ATTEN_CHL * amounts_on_chip[:, 0]
    cumul = level_prefix(atten, layer_tally)
    top = surface * jnp.exp(-(cumul - atten))
    bottom = surface * jnp.exp(-cumul)
    heat = (valid * (top - bottom)).astype(jnp.bfloat16)
    growth = jnp.exp(GROWTH_TEMP * temp_flat.astype(jnp.float32)) * top / (top + 1.0)
    mixed = jnp.einsum(
        "rs,nsf->nrf", reaction_rates, amounts_on_chip, precision=lax.Precision.HIGHEST
    )
    flux = (kappa_flat.astype(jnp.float32) * active)[:, None] * (
        level_below(amounts_on_chip) - amounts_on_chip
    )
    new = amounts_on_chip + valid[:, None] * STEP_DT * (
        flux - level_above_zero(flux) + growth[:, None] * mixed
    )
    return (new, heat)


def plane_blocks(field, blocks_x, blocks_y):
    return (
        field.reshape(blocks_x, 8, blocks_y, 8)
        .transpose(0, 2, 1, 3)
        .reshape(blocks_x * blocks_y, 64)
    )


def on_device(
    thermal_anomaly,
    ambient_diffusion,
    solar_light,
    sea_tile_flags,
    flooded_layer_tally,
    tile_holder_rank,
    solute_amounts,
    reaction_rates,
):
    layer_tally = thermal_anomaly.shape[0]
    span_east = thermal_anomaly.shape[1]
    span_north = thermal_anomaly.shape[2]
    blocks_x = span_east // 8
    blocks_y = span_north // 8
    tile_summation = blocks_x * blocks_y
    flat_width = layer_tally * 64
    depth_block = (sea_tile_flags * flooded_layer_tally).reshape(tile_summation)
    cell_count = jnp.repeat(
        jnp.repeat(depth_block.reshape(blocks_x, blocks_y), 8, axis=0), 8, axis=1
    )
    level_idx = lax.broadcasted_iota(jnp.int32, (layer_tally, 1, 1), 0)
    within_layer = (level_idx < cell_count[None]).astype(jnp.float32)
    piled_tiles = jnp.stack([thermal_anomaly, within_layer])
    padded = with_halo(piled_tiles, (("gx", 2), ("gy", 3)), 1)
    advanced_verticals = masked_step(padded[0], padded[1])
    dispatched = advanced_verticals.astype(jnp.bfloat16)
    thermal_tiles = (
        dispatched.reshape(layer_tally, blocks_x, 8, blocks_y, 8)
        .transpose(1, 3, 0, 2, 4)
        .reshape(tile_summation, flat_width)
    )
    ambient_diffusion_tiles = plane_blocks(ambient_diffusion, blocks_x, blocks_y)
    shortwave_blocks = plane_blocks(solar_light, blocks_x, blocks_y)
    diffusion_each_tile = flat_mixer(
        thermal_tiles.astype(jnp.float32),
        spread_levels(ambient_diffusion_tiles.astype(jnp.float32), layer_tally),
    )
    payload = jnp.concatenate([thermal_tiles, diffusion_each_tile, shortwave_blocks], axis=1)
    holder_chip = tile_holder_rank.reshape(tile_summation)
    order = jnp.arange(tile_summation, dtype=jnp.int32)
    same = (holder_chip[:, None] == holder_chip[None, :]) & (order[None, :] < order[:, None])
    rank = jnp.sum(same.astype(jnp.int32), axis=1)
    position_summation = solute_amounts.shape[2]
    device_groups = lax.axis_size("gy")
    slot_limit = position_summation // device_groups
    target_owner = holder_chip * slot_limit + rank
    selection_mask = (
        lax.broadcasted_iota(jnp.int32, (position_summation, tile_summation), 0)
        == target_owner[None, :]
    )
    select_b = selection_mask.astype(jnp.bfloat16)
    packed = jnp.einsum("sb,bf->sf", select_b, payload, preferred_element_type=jnp.float32).astype(
        jnp.bfloat16
    )
    packed_count = jnp.sum(selection_mask.astype(jnp.int32) * depth_block[None, :], axis=1)
    arrived_tiles, received_count = (
        lax.all_to_all(
            packed.reshape(device_groups, slot_limit, packed.shape[1]),
            "gy",
            split_axis=0,
            concat_axis=0,
            tiled=True,
        ),
        lax.all_to_all(
            packed_count.reshape(device_groups, slot_limit),
            "gy",
            split_axis=0,
            concat_axis=0,
            tiled=True,
        ),
    )
    arrived_tiles = arrived_tiles.reshape(position_summation, arrived_tiles.shape[2])
    tile_amount = received_count.reshape(position_summation)
    thermal_at_position = arrived_tiles[:, :flat_width]
    diffusion_at_position = arrived_tiles[:, flat_width : 2 * flat_width]
    solar_at_position = arrived_tiles[:, 2 * flat_width :]
    surface = spread_levels(solar_at_position.astype(jnp.float32), layer_tally)
    amounts_on_chip = solute_amounts.reshape(
        position_summation, solute_amounts.shape[3], flat_width
    )
    valid, active = flat_validity(tile_amount, flat_width)
    old_local = totals(amounts_on_chip, valid)
    cells_local = jnp.sum(valid)
    old_total, cells = lax.psum((old_local, cells_local), ("gx", "gy"))
    new, heat = column_step(
        thermal_at_position,
        diffusion_at_position,
        surface,
        valid,
        active,
        amounts_on_chip,
        reaction_rates,
        layer_tally,
    )
    new_total = lax.psum(totals(new, valid), ("gx", "gy"))
    shift = (old_total - new_total) / jnp.maximum(cells, 1.0)
    solute_final = jnp.where(
        valid[:, None] > 0, new + shift[None, :, None], amounts_on_chip
    ).reshape(solute_amounts.shape)
    returned_blocks = lax.all_to_all(
        heat.reshape(device_groups, slot_limit, flat_width),
        "gy",
        split_axis=0,
        concat_axis=0,
        tiled=True,
    )
    returned_blocks = returned_blocks.reshape(position_summation, flat_width)
    heat_blocks = jnp.einsum(
        "sb,sf->bf", select_b, returned_blocks, preferred_element_type=jnp.float32
    )
    warming_each_site = (
        heat_blocks.reshape(blocks_x, blocks_y, layer_tally, 8, 8)
        .transpose(2, 0, 3, 1, 4)
        .reshape(layer_tally, span_east, span_north)
    )
    thermal_final = advanced_verticals + WARMING_SCALE * warming_each_site
    return (thermal_final, solute_final)


def solution(mesh):
    return jax.shard_map(
        on_device,
        mesh=mesh,
        in_specs=(
            P(None, "gx", "gy"),
            P("gx", "gy"),
            P("gx", "gy"),
            P("gx", "gy", None),
            P("gx", "gy", None),
            P("gx", "gy", None, None),
            P("gx", "gy", None, None, None),
            P(),
        ),
        out_specs=(P(None, "gx", "gy"), P("gx", "gy", None, None, None)),
        check_vma=False,
    )
```

profile of v0, /device:TPU:0, one launch (start us, length us, event | category | flops | bytes accessed | tf_op | source)
XLA Modules:
  0.0 186.1 jit_solution(9731067672512701590)
XLA Ops:
  0.6 0.9 convert_reduce_fusion
  1.6 0.7 multiply_add_fusion
  2.2 0.7 multiply_bitcast_fusion.1
  3.0 0.7 all_to_all.12
  3.7 7.3 %all-to-all-start = ((s32[8,1,16]{2,1,0:T(1,128)}), s32[8,1,16]{2,1,0:T(1,128)S(1)}, u32[]{:S(2)}, u32[]{:S(2)}) async-start(s32[8,1,16]{2,1,0:T(1,128)} %bitcast.10), calls=%async_computation | async-start | bytes 8192 | tf_op jit(solution)/shard_map/all_to_all | solution.py:178
  11.3 1.2 pad_maximum_fusion.1
  12.5 2.7 %copy.128 = f32[2,32,32,128]{1,3,2,0:T(8,128)} copy(f32[2,32,32,128]{3,2,1,0:T(8,128)S(1)} %pad_maximum_fusion.1) | data formatting | bytes 2097152 | tf_op jit(solution)/shard_map/stack | solution.py:137
  15.2 1.1 fusion.39
  16.3 1.6 collective-permute-start
  17.9 1.3 collective-permute-start.1
  19.2 4.8 %fusion.18 = f32[128,1,2048]{2,1,0:T(1,128)S(1)} fusion(f32[128,8,2048]{2,1,0:T(8,128)} %bitcast.79), kind=kLoop, calls=%fused_computation.37 | loop fusion | flops 524288 | bytes 2097152 | tf_op jit(solution)/shard_map/add | solution.py:88
  24.0 0.3 copy.161
  24.7 1.3 collective-permute-start.3
  25.9 4.5 %collective-permute-start.2 = (f32[2,32,34,1]{2,1,3,0:T(8,128)S(1)}, f32[2,32,34,1]{2,1,3,0:T(8,128)S(1)}, u32[]{:S(2)}, u32[]{:S(2)}) collective-permute-start(f32[2,32,34,1]{2,1,3,0:T(8,128)S(1)} %copy.131), channel_id=1, source_target_pairs={{0,1},{1,2},{2,3},{3,4},{4,5},{5,6},{6,7},{8,9},{9,10},{10,11},{11... | collective-permute-start | bytes 26120 | tf_op jit(solution)/shard_map/ppermute | solution.py:22
  30.5 0.5 pad_add_fusion.4
  31.3 0.7 reshape.245
  32.5 0.9 copy.134
  33.4 2.7 %pad_maximum_fusion = f32[2,32,34,130]{1,3,2,0:T(8,128)S(1)} fusion(f32[2,32,34,1]{1,3,2,0:T(1,128)S(1)} %copy.134, f32[2,32,1,128]{1,3,2,0:T(8,128)S(1)} %collective-permute-done.1, f32[2,32,32,128]{1,3,2,0:T(8,128)} %copy.128, f32[2,32,1,128]{1,3,2,0:T(8,128)S(1)} %collective-permute-done, f32[2,32,34,1]{1,3,2,0:T(1,128)S(1)} %copy.133), kind=kLoop, calls=%fused_computation.9 | loop fusion | flops 1131520 | bytes 2263040 | tf_op jit(solution)/shard_map/concatenate | solution.py:20
  36.1 0.3 slice_bitcast_fusion
  36.4 3.6 %fusion.37 = (bf16[32,32,128]{0,2,1:T(8,128)(2,1)}, f32[32,32,128]{0,2,1:T(8,128)}) fusion(f32[32,34,130]{0,2,1:T(8,128)S(1)} %get-tuple-element.24, f32[32,34,130]{0,2,1:T(8,128)S(1)} %get-tuple-element.23), kind=kLoop, calls=%fused_computation.87 | loop fusion | flops 1966080 | bytes 6029312 | tf_op jit(solution)/shard_map/convert_element_type | solution.py:140
  40.0 4.9 %copy.136 = bf16[4,16,32,8,8]{1,0,4,3,2:T(4,128)(2,1)S(1)} copy(bf16[4,16,32,8,8]{2,4,1,3,0:T(8,128)(2,1)} %bitcast.87) | data formatting | bytes 524288 | tf_op jit(solution)/shard_map/transpose | solution.py:143
  45.0 1.8 reshape.243
  46.7 0.8 slice.135
  47.5 1.1 slice.134
  48.7 0.3 fusion.23
  48.9 1.5 convolution_convert_fusion
  50.4 2.5 %copy.139 = bf16[128,4160]{1,0:T(8,128)(2,1)} copy(bf16[128,4160]{0,1:T(8,128)(2,1)} %convolution_convert_fusion) | data formatting | bytes 2129920 | tf_op jit(solution)/shard_map/convert_element_type | solution.py:166
  53.0 6.3 %all-to-all-start.1 = ((bf16[8,16,4160]{2,1,0:T(8,128)(2,1)}), bf16[8,16,4160]{2,1,0:T(8,128)(2,1)}, u32[]{:S(2)}, u32[]{:S(2)}) async-start(bf16[8,16,4160]{2,1,0:T(8,128)(2,1)} %bitcast.86), calls=%async_computation.1 | async-start | bytes 2162688 | tf_op jit(solution)/shard_map/all_to_all | solution.py:171
  59.4 2.1 %slice.145 = f32[128,8,64]{2,1,0:T(8,128)} slice(f32[128,8,2048]{2,1,0:T(8,128)} %bitcast.80), slice={[0:128], [0:8], [1984:2048]} | slice | bytes 524288 | tf_op jit(solution)/shard_map/slice | solution.py:45
  61.5 9.0 %slice.144 = f32[128,8,1984]{2,1,0:T(8,128)} slice(f32[128,8,2048]{2,1,0:T(8,128)} %bitcast.81), slice={[0:128], [0:8], [64:2048]} | slice | bytes 16252928 | tf_op jit(solution)/shard_map/slice | solution.py:45
  70.9 0.8 slice.142
  71.8 0.5 broadcast.192
  72.3 0.6 reduce.7
  72.9 1.3 fusion.25
  74.2 12.9 %all-to-all-done.1 = bf16[8,16,4160]{2,1,0:T(8,128)(2,1)} async-done(((bf16[8,16,4160]{2,1,0:T(8,128)(2,1)}), bf16[8,16,4160]{2,1,0:T(8,128)(2,1)}, u32[]{:S(2)}, u32[]{:S(2)}) %all-to-all-start.1) | async-done | bytes 1064992 | tf_op jit(solution)/shard_map/all_to_all | solution.py:171
  87.1 0.8 slice.136
  88.1 1.4 copy.141
  89.5 4.6 %add_divide_fusion = (f32[128,2048]{1,0:T(8,128)S(1)}, bf16[128,2048]{1,0:T(8,128)(2,1)}, f32[128,2048]{1,0:T(8,128)}, f32[]{:T(128)}, f32[128,2048]{1,0:T(8,128)}) fusion(f32[128,2048]{1,0:T(8,128)} %copy.141, f32[128,2048]{1,0:T(8,128)S(1)} %pad_add_fusion.1, f32[128,1024]{1,0:T(8,128)} %slice.142, bf16[128,4160]{1,0:T(8,128)(2,1)} %bitcast.17, ...), kind=kLoop, calls=%fused_computation.46 | loop fusion | flops 5505023 | bytes 8405508 | tf_op jit(solution)/shard_map/div | solution.py:93
  94.1 3.7 %all-to-all-start.2 = ((bf16[8,16,2048]{2,1,0:T(8,128)(2,1)}), bf16[8,16,2048]{2,1,0:T(8,128)(2,1)S(1)}, u32[]{:S(2)}, u32[]{:S(2)}) async-start(bf16[8,16,2048]{2,1,0:T(8,128)(2,1)} %bitcast.90), calls=%async_computation.2 | async-start | bytes 1048576 | tf_op jit(solution)/shard_map/all_to_all | solution.py:214
  97.9 11.1 %fusion = f32[128,8,2048]{2,1,0:T(8,128)} fusion(f32[128,8,64]{2,1,0:T(8,128)} %slice.145, f32[128,8,1984]{2,1,0:T(8,128)} %slice.144, f32[128,2048]{1,0:T(8,128)} %get-tuple-element.31, f32[1,1,128,8,2048]{4,3,2,1,0:T(8,128)} %param.14), kind=kLoop, calls=%fused_computation.1 | loop fusion | flops 6291456 | bytes 26214400 | tf_op jit(solution)/shard_map/mul | solution.py:97
  109.1 21.6 %multiply_reduce_fusion = (f32[8]{0:T(128)S(1)}, f32[8]{0:T(128)S(1)}, f32[128,8,2048]{2,1,0:T(8,128)}) fusion(f32[128,2048]{1,0:T(8,128)S(1)} %copy-done.7, f32[1,1,128,8,2048]{4,3,2,1,0:T(8,128)S(1)} %bitcast.83, f32[8,8]{1,0:T(8,128)S(1)} %copy-done, f32[128,2048]{1,0:T(8,128)S(1)} %get-tuple-element.29, f32[128,8,2048]{2,1,0:T(8,128)} %fusion, ...), kind=kOutput, calls=%fused_computation.6 | convolution fusion | flops 220200944 | bytes 36438336 | tf_op jit(solution)/shard_map/rs,nsf->nrf/dot_general | solution.py:94
  130.8 40.8 %all-reduce.6 = (f32[8]{0:T(128)S(1)}, f32[8]{0:T(128)S(1)}, f32[]{:T(128)}) all-reduce(f32[8]{0:T(128)S(1)} %get-tuple-element.17, f32[8]{0:T(128)S(1)} %get-tuple-element.16, f32[]{:T(128)} %get-tuple-element.32), channel_id=1, replica_groups=mesh['gx'=4,'gy'=8] {'gx','gy'}, use_global_device_ids=true, to_apply=%region_3.4 | all-reduce | flops 17 | bytes 136 | tf_op jit(solution)/shard_map/psum | solution.py:198
  172.2 9.3 %select_bitcast_fusion = f32[1,1,128,8,2048]{4,3,2,1,0:T(8,128)} fusion(f32[128,8,2048]{2,1,0:T(8,128)} %get-tuple-element.38, f32[8]{0:T(128)S(1)} %subtract_divide_fusion, pred[128,2048]{1,0:T(8,128)(4,1)S(1)} %get-tuple-element.34, f32[1,1,128,8,2048]{4,3,2,1,0:T(8,128)} %param.14), kind=kLoop, calls=%fused_computation.5 | loop fusion | flops 4194304 | bytes 25428000 | tf_op jit(solution)/shard_map/reshape | solution.py:213
  181.5 0.3 copy.143
  181.8 1.0 multiply_bitcast_fusion
  182.8 0.9 copy.145
  183.7 0.7 copy-done.4
  184.6 1.5 copy.146
  (62 shorter events, 2.7 us)
Async XLA Ops:
  0.6 108.4 %copy-start = (f32[8,8]{1,0:T(8,128)S(1)}, f32[8,8]{1,0:T(8,128)}, u32[]{:S(2)}) copy-start(f32[8,8]{1,0:T(8,128)} %param.15) | copy-start | bytes 772
  3.7 49.3 %all-to-all-start = ((s32[8,1,16]{2,1,0:T(1,128)}), s32[8,1,16]{2,1,0:T(1,128)S(1)}, u32[]{:S(2)}, u32[]{:S(2)}) async-start(s32[8,1,16]{2,1,0:T(1,128)} %bitcast.10), calls=%async_computation | async-start | bytes 8192 | tf_op jit(solution)/shard_map/all_to_all | solution.py:178
  15.2 9.2 %copy-start.1 = (f32[2,32,32,128]{1,3,2,0:T(8,128)S(1)}, f32[2,32,32,128]{1,3,2,0:T(8,128)}, u32[]{:S(2)}) copy-start(f32[2,32,32,128]{1,3,2,0:T(8,128)} %copy.128) | copy-start | bytes 3145732
  16.3 8.0 %collective-permute-start = (f32[2,32,1,128]{1,3,2,0:T(8,128)S(1)}, f32[2,32,1,128]{1,3,2,0:T(8,128)S(1)}, u32[]{:S(2)}, u32[]{:S(2)}) collective-permute-start(f32[2,32,1,128]{1,3,2,0:T(8,128)S(1)} %get-tuple-element.27), channel_id=1, source_target_pairs={{0,8},{8,16},{16,24},{1,9},{9,17},{17,25},{2,10},{10,18},{18,26},{... | collective-permute-start | bytes 98312 | tf_op jit(solution)/shard_map/ppermute | solution.py:22
  17.9 6.4 %collective-permute-start.1 = (f32[2,32,1,128]{1,3,2,0:T(8,128)S(1)}, f32[2,32,1,128]{1,3,2,0:T(8,128)S(1)}, u32[]{:S(2)}, u32[]{:S(2)}) collective-permute-start(f32[2,32,1,128]{1,3,2,0:T(8,128)S(1)} %get-tuple-element.28), channel_id=1, source_target_pairs={{8,0},{16,8},{24,16},{9,1},{17,9},{25,17},{10,2},{18,10},{26,18},{... | collective-permute-start | bytes 98312 | tf_op jit(solution)/shard_map/ppermute | solution.py:24
  24.5 6.5 %copy-start.9 = (bf16[32,128]{1,0:T(8,128)(2,1)S(1)}, bf16[32,128]{1,0:T(8,128)(2,1)}, u32[]{:S(2)}) copy-start(bf16[32,128]{1,0:T(8,128)(2,1)} %param.10) | copy-start | bytes 24580
  24.5 7.6 %copy-start.10 = (bf16[32,128]{1,0:T(8,128)(2,1)S(1)}, bf16[32,128]{1,0:T(8,128)(2,1)}, u32[]{:S(2)}) copy-start(bf16[32,128]{1,0:T(8,128)(2,1)} %param.9) | copy-start | bytes 24580
  24.7 7.8 %collective-permute-start.3 = (f32[2,32,34,1]{2,1,3,0:T(8,128)S(1)}, f32[2,32,34,1]{2,1,3,0:T(8,128)}, u32[]{:S(2)}, u32[]{:S(2)}) collective-permute-start(f32[2,32,34,1]{2,1,3,0:T(8,128)S(1)} %copy.132), channel_id=1, source_target_pairs={{1,0},{2,1},{3,2},{4,3},{5,4},{6,5},{7,6},{9,8},{10,9},{11,10},{12... | collective-permute-start | bytes 26120 | tf_op jit(solution)/shard_map/ppermute | solution.py:24
  25.9 7.4 %collective-permute-start.2 = (f32[2,32,34,1]{2,1,3,0:T(8,128)S(1)}, f32[2,32,34,1]{2,1,3,0:T(8,128)S(1)}, u32[]{:S(2)}, u32[]{:S(2)}) collective-permute-start(f32[2,32,34,1]{2,1,3,0:T(8,128)S(1)} %copy.131), channel_id=1, source_target_pairs={{0,1},{1,2},{2,3},{3,4},{4,5},{5,6},{6,7},{8,9},{9,10},{10,11},{11... | collective-permute-start | bytes 26120 | tf_op jit(solution)/shard_map/ppermute | solution.py:22
  31.0 5.1 %copy-start.2 = (f32[128,2048]{1,0:T(8,128)}, f32[128,2048]{1,0:T(8,128)S(1)}, u32[]{:S(2)}) copy-start(f32[128,2048]{1,0:T(8,128)S(1)} %pad_add_fusion.4) | copy-start | bytes 3145732
  46.7 1.9 %copy-start.5 = (bf16[64,2048]{0,1:T(8,128)(2,1)S(1)}, bf16[64,2048]{0,1:T(8,128)(2,1)}, u32[]{:S(2)}) copy-start(bf16[64,2048]{0,1:T(8,128)(2,1)} %reshape.243) | copy-start | bytes 786436
  46.7 2.2 %copy-start.8 = (bf16[64,64]{0,1:T(8,128)(2,1)S(1)}, bf16[64,64]{0,1:T(8,128)(2,1)}, u32[]{:S(2)}) copy-start(bf16[64,64]{0,1:T(8,128)(2,1)} %reshape.245) | copy-start | bytes 24580
  50.4 8.9 %copy-start.3 = (f32[128,2048]{1,0:T(8,128)S(1)}, f32[128,2048]{1,0:T(8,128)}, u32[]{:S(2)}) copy-start(f32[128,2048]{1,0:T(8,128)} %copy-done.2) | copy-start | bytes 3145732
  50.4 8.9 %slice-start.2 = ((f32[128,2048]{1,0:T(8,128)}), f32[128,1920]{1,0:T(8,128)S(1)}, s32[]{:S(2)}) async-start(f32[128,2048]{1,0:T(8,128)} %copy-done.2), calls=%async_computation.5 | async-start | bytes 1966080 | tf_op jit(solution)/shard_map/slice | solution.py:57
  53.0 34.2 %all-to-all-start.1 = ((bf16[8,16,4160]{2,1,0:T(8,128)(2,1)}), bf16[8,16,4160]{2,1,0:T(8,128)(2,1)}, u32[]{:S(2)}, u32[]{:S(2)}) async-start(bf16[8,16,4160]{2,1,0:T(8,128)(2,1)} %bitcast.86), calls=%async_computation.1 | async-start | bytes 2162688 | tf_op jit(solution)/shard_map/all_to_all | solution.py:171
  94.1 87.4 %all-to-all-start.2 = ((bf16[8,16,2048]{2,1,0:T(8,128)(2,1)}), bf16[8,16,2048]{2,1,0:T(8,128)(2,1)S(1)}, u32[]{:S(2)}, u32[]{:S(2)}) async-start(bf16[8,16,2048]{2,1,0:T(8,128)(2,1)} %bitcast.90), calls=%async_computation.2 | async-start | bytes 1048576 | tf_op jit(solution)/shard_map/all_to_all | solution.py:214
  97.8 11.2 %slice-start = ((s8[8388608]{0:T(1024)(128)(4,1)}), s8[4194304]{0:T(1024)(128)(4,1)S(1)}, s32[]{:S(2)}) async-start(s8[8388608]{0:T(1024)(128)(4,1)} %bitcast.82), calls=%async_computation.3 | async-start | bytes 8388608
  97.8 11.2 %slice-start.1 = ((s8[8388608]{0:T(1024)(128)(4,1)}), s8[4194304]{0:T(1024)(128)(4,1)S(1)}, s32[]{:S(2)}) async-start(s8[8388608]{0:T(1024)(128)(4,1)} %bitcast.82), calls=%async_computation.4 | async-start | bytes 8388608
  97.9 11.2 %copy-start.6 = (f32[128,2048]{1,0:T(8,128)S(1)}, f32[128,2048]{1,0:T(8,128)}, u32[]{:S(2)}) copy-start(f32[128,2048]{1,0:T(8,128)} %get-tuple-element.33) | copy-start | bytes 3145732
  97.9 11.3 %copy-start.7 = (f32[128,2048]{1,0:T(8,128)S(1)}, f32[128,2048]{1,0:T(8,128)}, u32[]{:S(2)}) copy-start(f32[128,2048]{1,0:T(8,128)} %get-tuple-element.35) | copy-start | bytes 3145732
  182.8 1.6 copy-start.4
where the time goes:
time: 187 us; the launch traced here: 186 us
  other arithmetic  43 us (23%)
  blocking collectives  40.8 us (22%)
  local copies, waits for them, and re-layouts  37.5 us (20%)
  starting transfers between devices  26.1 us (14%)
  matrix products  24.1 us (13%)
  waiting for transfers between devices  12.9 us (7%)
    psum x1, blocking collectives, on_device(): old_total, cells = lax.psum((old_local, cells_local), ('gx', 'gy'))  40.8 us
    dot_general x1, matrix products, column_step(): jnp.einsum('rs,nsf->nrf', reaction_rates, amounts_on_chip, precision=lax....  21.6 us
    slice x4, local copies, waits for them, and re-layouts, level_below(): return jnp.concatenate([values[..., 64:], values[..., -64:]], axis=-1)  13 us
    all_to_all x1, waiting for transfers between devices, on_device(): lax.all_to_all(packed.reshape(device_groups, slot_limit, packed.shape[1])...  12.9 us
    mul x1, other arithmetic, column_step(): (kappa_flat.astype(jnp.float32) * active)[:, None]  11.1 us
    reshape x1, other arithmetic, on_device(): solute_final = jnp.where(valid[:, None] > 0, new + shift[None, :, None],...  9.28 us
    all_to_all x1, starting transfers between devices, on_device(): lax.all_to_all(packed_count.reshape(device_groups, slot_limit), 'gy', spl...  7.28 us
    all_to_all x1, starting transfers between devices, on_device(): lax.all_to_all(packed.reshape(device_groups, slot_limit, packed.shape[1])...  6.32 us
  transfers between devices with their start and end apart: 7, of which 1 were waited for; matrix products, arithmetic and copies ran while one was open for 48% of the time, Pallas kernels for 0%

commit v1 on v0

v1 whole, which is shorter than its diff:
```python
import functools
import jax
import jax.numpy as jnp
from jax import lax
from jax.experimental import pallas as pl
from jax.experimental.pallas import tpu as pltpu
from jax.sharding import PartitionSpec as P

NU_COEF = 0.2
STEP_DT = 0.05
ATTEN_WATER = 0.06
ATTEN_CHL = 0.05
WARMING_SCALE = 0.5
GROWTH_TEMP = 0.063
LANES = 128
HALF = 64
SUB = 8


f32 = jnp.float32
bf16 = jnp.bfloat16


def iota(shape, dim):
    return lax.broadcasted_iota(jnp.int32, shape, dim)


def swap_granules(x):
    row = iota(x.shape, 1)
    lane = iota(x.shape, 2)
    for step in (1, 2, 4):
        r = (row & step) != 0
        c = (lane & (step * SUB)) != 0
        w = step * SUB
        up = pltpu.roll(pltpu.roll(x, SUB - step, 1), w, 2)
        down = pltpu.roll(pltpu.roll(x, step, 1), LANES - w, 2)
        x = jnp.where(r == c, x, jnp.where(c, up, down))
    return x


def join_levels(a, b):
    low = iota(a.shape, 2) < HALF
    return (
        jnp.where(low, a, pltpu.roll(b, HALF, 2)),
        jnp.where(low, pltpu.roll(a, HALF, 2), b),
    )


def row_of(ref, *at, n=SUB):
    return ref[(*at[:-1], pl.ds(at[-1], n, stride=0), slice(None))]


def depth_rows(depth, blocks_y):
    n = depth.shape[1]
    mine = iota((SUB, n), 1) // blocks_y == iota((SUB, n), 0)
    left = jnp.where(mine, jnp.broadcast_to(depth, (SUB, n)), 0.0)
    spread = iota((n, LANES), 0) % blocks_y == iota((n, LANES), 1) // SUB
    return jnp.dot(left, spread.astype(f32), preferred_element_type=f32)


def edge_depth(depth, blocks_x, blocks_y, by):
    n = depth.shape[1]
    pick = iota((n, LANES), 0) == (iota((n, LANES), 1) % blocks_x) * blocks_y + by
    return jnp.dot(
        jnp.broadcast_to(depth, (SUB, n)), pick.astype(f32), preferred_element_type=f32
    )


def edges_kernel(bx_n, by_n, *refs):
    sources, (xlo, xhi, ylo, yhi), held, sems = refs[:6], refs[6:10], refs[10:16], refs[16]
    t, flags, tally = held[:3]
    levels, nx, _ = t.shape
    loads = [
        pltpu.make_async_copy(x, y, sems.at[i]) for i, (x, y) in enumerate(zip(sources, held))
    ]
    for load in loads:
        load.start()
    for load in loads:
        load.wait()
    depth = (flags[...] * tally[...]).astype(f32)
    d = depth_rows(depth, by_n)
    for k in range(levels):
        xlo[k : k + 1, :] = t[k, 0:1, :]
        xhi[k : k + 1, :] = t[k, nx - 1 : nx, :]
    xlo[levels : levels + SUB, :] = jnp.broadcast_to(d[0:1], (SUB, LANES))
    xhi[levels : levels + SUB, :] = jnp.broadcast_to(d[bx_n - 1 : bx_n], (SUB, LANES))
    lane = iota((SUB, LANES), 1)
    lo = jnp.zeros((SUB, LANES), f32)
    hi = jnp.zeros((SUB, LANES), f32)
    for k0 in range(0, levels, 4):
        places = [(k, bx) for k in range(k0, k0 + 4) for bx in range(bx_n)]
        tiles = [t[k, bx * SUB : (bx + 1) * SUB, :] for k, bx in places]
        js = [k * bx_n + bx for k, bx in places]
        los = [pltpu.roll(v, j, 1) for v, j in zip(tiles, js)]
        his = [pltpu.roll(v, (j + 1) % LANES, 1) for v, j in zip(tiles, js)]
        for j, a, b in zip(js, los, his):
            lo = jnp.where(lane == j, a, lo)
            hi = jnp.where(lane == j, b, hi)
    ylo[0:SUB, :] = lo
    yhi[0:SUB, :] = hi
    k_lane = (lane // bx_n).astype(f32)
    ylo[SUB:, :] = (k_lane < edge_depth(depth, bx_n, by_n, 0)).astype(f32)
    yhi[SUB:, :] = (k_lane < edge_depth(depth, bx_n, by_n, by_n - 1)).astype(f32)


def slots_kernel(bx_n, by_n, cap, n_gy, amb, light, flags, tally, holder, sel, sel_t, tail):
    n = bx_n * by_n
    slots = sel.shape[0]
    me = lax.axis_index("gy").astype(f32)
    own = holder[...].astype(f32)
    row_i = iota((n, n), 0)
    col_i = iota((n, n), 1)
    own_row = jnp.broadcast_to(own, (n, n))
    own_col = jnp.sum(jnp.where(row_i == col_i, own_row, 0.0), axis=1, keepdims=True)
    same = own_row == own_col
    rank_row = jnp.sum(jnp.where(same & (row_i < col_i), 1.0, 0.0), axis=0, keepdims=True)
    rank_col = jnp.sum(jnp.where(same & (col_i < row_i), 1.0, 0.0), axis=1, keepdims=True)
    to_row = own * cap + rank_row
    back = me - own_col
    back = jnp.where(back < 0, back + n_gy, back)
    to_col = back * cap + rank_col
    chosen = (iota((slots, n), 0).astype(f32) == to_row).astype(bf16)
    sel[...] = chosen
    sel_t[...] = (iota((n, slots), 1).astype(f32) == to_col).astype(bf16)
    depth = (flags[...] * tally[...]).astype(f32)
    depth_col = jnp.sum(
        jnp.where(row_i == col_i, jnp.broadcast_to(depth, (n, n)), 0.0), axis=1, keepdims=True
    )
    a = amb[...].astype(f32).reshape(bx_n, SUB, LANES)
    b = light[...].astype(f32).reshape(bx_n, SUB, LANES)
    halves = jnp.stack(join_levels(a, b), axis=1).reshape(2 * bx_n, SUB, LANES)
    rows = swap_granules(halves).reshape(n, LANES)
    fields = jnp.concatenate([rows, jnp.broadcast_to(depth_col, (n, LANES))], axis=1).astype(bf16)
    tail[...] = jnp.dot(chosen, fields, preferred_element_type=f32).astype(bf16)


def stencil_kernel(
    bx_n, by_n, t, flags, tally, fxlo, fxhi, fylo, fyhi, own_lo, own_hi, sel, tail,
    stepped, packed, blocks,
):
    levels = t.shape[0]
    width = levels * HALF
    depth = (flags[...] * tally[...]).astype(f32)
    d = depth_rows(depth, by_n)
    nx = t.shape[1]
    lane = iota((nx, LANES), 1)
    row = iota((nx, LANES), 0)
    d_lo = jnp.broadcast_to(fxlo[levels : levels + 1, :], (nx, LANES))
    d_hi = jnp.broadcast_to(fxhi[levels : levels + 1, :], (nx, LANES))
    d_at = jnp.concatenate(
        [jnp.broadcast_to(d[bx : bx + 1], (SUB, LANES)) for bx in range(bx_n)], axis=0
    )
    d_xm = jnp.where(row == 0, d_lo, pltpu.roll(d_at, 1, 0))
    d_xp = jnp.where(row == nx - 1, d_hi, pltpu.roll(d_at, nx - 1, 0))
    d_ym = jnp.where(lane == 0, 0.0, pltpu.roll(d_at, 1, 1))
    d_yp = jnp.where(lane == LANES - 1, 0.0, pltpu.roll(d_at, LANES - 1, 1))
    add_lo = fylo[SUB:, :] * (fylo[0:SUB, :] - own_lo[0:SUB, :])
    add_hi = fyhi[SUB:, :] * (fyhi[0:SUB, :] - own_hi[0:SUB, :])
    for k0 in range(0, levels, 4):
        done = []
        for k in range(k0, k0 + 4):
            kf = float(k)
            c = t[k]
            xm = jnp.where(row == 0, row_of(fxlo, k, n=nx), pltpu.roll(c, 1, 0))
            xp = jnp.where(row == nx - 1, row_of(fxhi, k, n=nx), pltpu.roll(c, nx - 1, 0))
            ym = pltpu.roll(c, 1, 1)
            yp = pltpu.roll(c, LANES - 1, 1)
            js = [k * bx_n + bx for bx in range(bx_n)]
            lo = jnp.concatenate([pltpu.roll(add_lo, (LANES - j) % LANES, 1) for j in js], axis=0)
            hi = jnp.concatenate(
                [pltpu.roll(add_hi, (LANES - 1 - j) % LANES, 1) for j in js], axis=0
            )
            total = jnp.where(d_xm > kf, xm - c, 0.0)
            total = total + jnp.where(d_xp > kf, xp - c, 0.0)
            total = total + jnp.where(lane == 0, lo, jnp.where(d_ym > kf, ym - c, 0.0))
            total = total + jnp.where(lane == LANES - 1, hi, jnp.where(d_yp > kf, yp - c, 0.0))
            s = c + jnp.where(d_at > kf, NU_COEF * total, 0.0)
            stepped[k] = s
            done.append(s.reshape(bx_n, SUB, LANES))
        halves = []
        for p in (0, 2):
            halves += list(join_levels(done[p], done[p + 1]))
        out = swap_granules(jnp.concatenate(halves, axis=0))
        for q in range(4):
            kp = k0 // 2 + q // 2
            for bx in range(bx_n):
                g = (bx * 2 + q % 2) * SUB
                blocks[g : g + SUB, kp * LANES : (kp + 1) * LANES] = out[q * bx_n + bx]
    packed[:, :width] = jnp.dot(
        sel[...], blocks[...].astype(bf16), preferred_element_type=f32
    ).astype(bf16)
    packed[:, width:] = tail[...]


def clear_kernel(n_gy, c, above, *rest):
    passed, (buf, sems) = rest[:n_gy], rest[n_gy:]
    cap = passed[0].shape[0]
    width = above.shape[1]
    me = lax.axis_index("gy")
    chunks = [lax.rem(me + i, n_gy) * cap for i in range(n_gy)]
    loads = [
        pltpu.make_async_copy(c.at[pl.ds(r, cap)], buf.at[i], sems.at[i])
        for i, r in enumerate(chunks)
    ]
    for load in loads:
        load.start()
    low = iota((cap, LANES), 1) < HALF
    spans = [slice(v * LANES, (v + 1) * LANES) for v in range(width // LANES)]
    for i, r in enumerate(chunks):
        loads[i].wait()
        a = [ATTEN_WATER + ATTEN_CHL * buf[i, :, 0, at] for at in spans]
        both = [x + pltpu.roll(x, HALF, 1) for x in a]
        carry = jnp.zeros((cap, LANES), f32)
        sums = []
        for x, y in zip(a, both):
            sums.append(carry + jnp.where(low, x, y))
            carry = carry + y
        left = [jnp.exp(-x) for x in sums]
        before = [jnp.ones((cap, LANES), f32)] + left[:-1]
        prev = [pltpu.roll(jnp.where(low, x, y), HALF, 1) for x, y in zip(left, before)]
        for at, x, y in zip(spans, prev, left):
            above[pl.ds(pl.multiple_of(r, cap), cap), at] = x
            passed[i][:, at] = (x - y).astype(bf16)


def spread_tail(arrived, rows, width):
    tail = arrived[rows, width : width + LANES].astype(f32)
    count = arrived[rows, width + LANES :].astype(f32)
    low = iota(tail.shape, 1) < HALF
    turned = pltpu.roll(tail, HALF, 1)
    return jnp.where(low, tail, turned), jnp.where(low, turned, tail), count


def chunk_loads(c, buf, sems):
    group = buf.shape[1]
    return [
        pltpu.make_async_copy(c.at[pl.ds(i * group, group)], buf.at[i], sems.at[i])
        for i in range(buf.shape[0])
    ]


def growth_kernel(arrived, above, c, weight, part, buf, sems):
    chunks, group, tracers, width = buf.shape
    for load in chunk_loads(c, buf, sems):
        load.start()
    spans = [slice(v * LANES, (v + 1) * LANES) for v in range(width // LANES)]
    half = (iota((group, LANES), 1) // HALF).astype(f32)

    def one(i, carry):
        sums, counts = list(carry[:-1]), carry[-1]
        r = pl.multiple_of(i * group, group)
        rows = pl.ds(r, group)
        _, light, count = spread_tail(arrived, rows, width)
        tops = [light * above[rows, at] for at in spans]
        temp = [jnp.exp(GROWTH_TEMP * arrived[rows, at].astype(f32)) for at in spans]
        rest = [1.0 / (x + 1.0) for x in tops]
        for v in range(len(spans)):
            g = STEP_DT * (temp[v] * (tops[v] * rest[v]))
            weight[v, rows, :] = jnp.where(half + float(2 * v) < count, g, 0.0)
        pltpu.make_async_copy(c.at[rows], buf.at[i], sems.at[i]).wait()
        for v, at in enumerate(spans):
            for s in range(group):
                sums[s % 8] = sums[s % 8] + row_of(weight, v, r + s) * buf[i, s, :, at]
        return (*sums, counts + count)

    start = (*[jnp.zeros((tracers, LANES), f32)] * 8, jnp.zeros((group, LANES), f32))
    *sums, counts = lax.fori_loop(0, chunks, one, start)
    total = functools.reduce(jnp.add, sums)
    total = total + pltpu.roll(total, HALF, 1)
    wet = jnp.broadcast_to(jnp.sum(counts, axis=0, keepdims=True), (tracers, LANES))
    line = jnp.where(iota((tracers, LANES), 1) < HALF, total, wet)
    part[...] = jnp.broadcast_to(line[None], part.shape)


def final_kernel(
    parts, arrived, weight, rates, c, out, buf, reactions, mix, mixed, fluxes, sems, out_sems
):
    chunks, group, tracers, width = buf.shape
    for load in chunk_loads(c, buf, sems):
        load.start()
    n_rows = group * tracers
    lane = iota((tracers, LANES), 1)
    steps = width // LANES
    spans = [slice(v * LANES, (v + 1) * LANES) for v in range(steps)]

    total = jnp.sum(parts[...], axis=0)
    grown = jnp.sum(jnp.where(lane < HALF, total, 0.0), axis=1, keepdims=True)
    cells = HALF * total[:, LANES - 1 :]
    change = jnp.zeros((tracers, LANES), f32)
    for s in range(tracers):
        change = change + rates[:, s : s + 1] * jnp.broadcast_to(
            grown[s : s + 1, :], (tracers, LANES)
        )
    move = (-change / jnp.maximum(cells, 1.0))[None]
    i_row = iota((n_rows, tracers), 0) % tracers == iota((n_rows, tracers), 1)
    j_col = iota((tracers, n_rows), 1) % tracers == iota((tracers, n_rows), 0)
    spread = jnp.dot(i_row.astype(f32), rates[...], preferred_element_type=f32)
    spread = jnp.dot(spread, j_col.astype(f32), preferred_element_type=f32)
    one_slot = iota((n_rows, n_rows), 0) // tracers == iota((n_rows, n_rows), 1) // tracers
    reactions[...] = jnp.where(one_slot, spread, 0.0).astype(bf16)

    half = (iota((group, LANES), 1) // HALF).astype(f32)
    low = iota((group, LANES), 1) < HALF
    low3 = iota((group, tracers, LANES), 2) < HALF

    def one(i, carry):
        r = pl.multiple_of(i * group, group)
        rows = pl.ds(r, group)
        amb, _, count = spread_tail(arrived, rows, width)
        here = [arrived[rows, at].astype(f32) for at in spans]
        below = [
            pltpu.roll(jnp.where(low, y, x), HALF, 1) for x, y in zip(here, here[1:] + here[-1:])
        ]
        bend = [jnp.tanh(x - y) for x, y in zip(here, below)]
        for v in range(steps):
            m = (amb * (1.0 + 0.5 * bend[v])).astype(bf16).astype(f32)
            mix[v] = jnp.where(half + float(2 * v + 1) < count, STEP_DT * m, 0.0)
        pltpu.make_async_copy(c.at[rows], buf.at[i], sems.at[i]).wait()
        mixed[...] = jnp.dot(
            reactions[...], buf[i].reshape(n_rows, width).astype(bf16), preferred_element_type=f32
        )

        def turned(v):
            nx = spans[min(v + 1, steps - 1)]
            return pltpu.roll(jnp.where(low3, buf[i, :, :, nx], buf[i, :, :, spans[v]]), HALF, 2)

        waiting = [turned(0), turned(1)]
        for v, at in enumerate(spans):
            if v + 2 < steps:
                waiting.append(turned(v + 2))
            spread_mix = jnp.stack([row_of(mix, v, s) for s in range(group)])
            fluxes[v] = spread_mix * (waiting.pop(0) - buf[i, :, :, at])

        def turned_flux(v):
            prev = fluxes[v - 1] if v else jnp.zeros((group, tracers, LANES), f32)
            return pltpu.roll(jnp.where(low3, fluxes[v], prev), HALF, 2)

        spare = count - half
        left = jnp.stack(
            [jnp.broadcast_to(spare[s : s + 1, :], (tracers, LANES)) for s in range(group)]
        )
        waiting = [turned_flux(0), turned_flux(1)]
        for v, at in enumerate(spans):
            if v + 2 < steps:
                waiting.append(turned_flux(v + 2))
            w = jnp.stack([row_of(weight, v, r + s) for s in range(group)])
            m = mixed[:, at].reshape(group, tracers, LANES)
            y = buf[i, :, :, at] + ((fluxes[v] - waiting.pop(0)) + w * m)
            buf[i, :, :, at] = y + jnp.where(left > float(2 * v), move, 0.0)
        pltpu.make_async_copy(buf.at[i], out.at[rows], out_sems.at[i]).start()
        return carry

    lax.fori_loop(0, chunks, one, 0)
    for i in range(chunks):
        pltpu.make_async_copy(buf.at[i], out.at[pl.ds(i * group, group)], out_sems.at[i]).wait()


def warm_kernel(bx_n, by_n, n_gy, sel_t, light, flags, tally, stepped, *rest):
    returned, (out, blocks) = rest[:n_gy], rest[n_gy:]
    levels, nx, ny = stepped.shape
    got = jnp.concatenate([r[...] for r in returned], axis=0)
    blocks[...] = jnp.dot(sel_t[...], got, preferred_element_type=f32)
    depth = (flags[...] * tally[...]).astype(f32)
    d = depth_rows(depth, by_n)
    d_at = jnp.concatenate(
        [jnp.broadcast_to(d[bx : bx + 1], (SUB, LANES)) for bx in range(bx_n)], axis=0
    )
    scale = WARMING_SCALE * light[...].astype(f32)
    for k0 in range(0, levels, 4):
        halves = []
        for q in range(4):
            kp = k0 // 2 + q // 2
            for bx in range(bx_n):
                g = (bx * 2 + q % 2) * SUB
                halves.append(blocks[g : g + SUB, kp * LANES : (kp + 1) * LANES])
        swapped = swap_granules(jnp.stack(halves))
        for p in range(2):
            lo = swapped[2 * p * bx_n : (2 * p + 1) * bx_n]
            hi = swapped[(2 * p + 1) * bx_n : (2 * p + 2) * bx_n]
            for e, took in enumerate(join_levels(lo, hi)):
                k = k0 + 2 * p + e
                out[k] = stepped[k] + jnp.where(d_at > float(k), scale * took.reshape(nx, ny), 0.0)


def vmem(n):
    return [pl.BlockSpec(memory_space=pltpu.VMEM)] * n


def shaped(shape, dtype):
    return jax.ShapeDtypeStruct(shape, dtype)


def params():
    return pltpu.CompilerParams(vmem_limit_bytes=20 << 20)


def in_hbm(x):
    return pltpu.with_memory_space_constraint(x, pltpu.HBM)


def on_device(
    thermal_anomaly,
    ambient_diffusion,
    solar_light,
    sea_tile_flags,
    flooded_layer_tally,
    tile_holder_rank,
    solute_amounts,
    reaction_rates,
):
    levels, nx, ny = thermal_anomaly.shape
    bx_n, by_n = nx // 8, ny // 8
    n_blocks = bx_n * by_n
    slots, tracers, width = solute_amounts.shape[2:]
    n_gy = lax.axis_size("gy")
    n_all = n_gy * lax.axis_size("gx")
    cap = slots // n_gy
    flags = sea_tile_flags.reshape(1, n_blocks)
    tally = flooded_layer_tally.reshape(1, n_blocks)
    holder = tile_holder_rank.reshape(1, n_blocks)
    amounts = in_hbm(solute_amounts.reshape(slots, tracers, width))

    sources = [thermal_anomaly, flags, tally, ambient_diffusion, solar_light, holder]
    xlo, xhi, ylo, yhi, *held = pl.pallas_call(
        functools.partial(edges_kernel, bx_n, by_n),
        out_shape=[shaped((levels + SUB, LANES), f32)] * 2
        + [shaped((2 * SUB, LANES), f32)] * 2
        + [shaped(x.shape, x.dtype) for x in sources],
        in_specs=[pl.BlockSpec(memory_space=pltpu.HBM)] * len(sources),
        out_specs=vmem(4 + len(sources)),
        scratch_shapes=[pltpu.SemaphoreType.DMA((len(sources),))],
        compiler_params=params(),
        name="edges",
    )(*[in_hbm(x) for x in sources])
    thermal, flags, tally, ambient, light, holder = held

    def onward(x, axis, way):
        count = lax.axis_size(axis)
        pairs = [(i, i + 1) for i in range(count - 1)]
        return lax.ppermute(x, axis, pairs if way > 0 else [(j, i) for i, j in pairs])

    fxlo = onward(xhi, "gx", 1)
    fxhi = onward(xlo, "gx", -1)
    fylo = onward(yhi, "gy", 1)
    fyhi = onward(ylo, "gy", -1)

    sel, sel_t, tail = pl.pallas_call(
        functools.partial(slots_kernel, bx_n, by_n, cap, n_gy),
        out_shape=[
            shaped((slots, n_blocks), bf16),
            shaped((n_blocks, slots), bf16),
            shaped((slots, 2 * LANES), bf16),
        ],
        in_specs=vmem(5),
        out_specs=vmem(3),
        compiler_params=params(),
        name="slots",
    )(ambient, light, flags, tally, holder)

    group = 16
    steps = slots // group
    buffers = [
        pltpu.VMEM((steps, group, tracers, width), f32),
        pltpu.SemaphoreType.DMA((steps,)),
    ]
    any_hbm = pl.BlockSpec(memory_space=pltpu.HBM)
    above, *passed = pl.pallas_call(
        functools.partial(clear_kernel, n_gy),
        out_shape=[shaped((slots, width), f32)] + [shaped((cap, width), bf16)] * n_gy,
        in_specs=[pl.BlockSpec(memory_space=pltpu.HBM)],
        out_specs=vmem(1 + n_gy),
        scratch_shapes=[
            pltpu.VMEM((n_gy, cap, tracers, width), f32),
            pltpu.SemaphoreType.DMA((n_gy,)),
        ],
        compiler_params=params(),
        name="clear",
    )(amounts)

    stepped, packed = pl.pallas_call(
        functools.partial(stencil_kernel, bx_n, by_n),
        out_shape=[shaped((levels, nx, ny), f32), shaped((slots, width + 2 * LANES), bf16)],
        in_specs=vmem(11),
        out_specs=vmem(2),
        scratch_shapes=[pltpu.VMEM((n_blocks, width), f32)],
        compiler_params=params(),
        name="stencil",
    )(thermal, flags, tally, fxlo, fxhi, fylo, fyhi, ylo, yhi, sel, tail)

    def exchange(x):
        y = lax.all_to_all(x.reshape(n_gy, cap, x.shape[1]), "gy", 0, 0, tiled=True)
        return y.reshape(x.shape)

    arrived = exchange(packed)
    returned = [passed[0]]
    for d in range(1, n_gy):
        pairs = [(i, (i + d) % n_gy) for i in range(n_gy)]
        returned.append(lax.ppermute(passed[d], "gy", pairs))

    weight, part = pl.pallas_call(
        growth_kernel,
        out_shape=[
            shaped((width // LANES, slots, LANES), f32),
            shaped((n_all, tracers, LANES), f32),
        ],
        in_specs=vmem(2) + [any_hbm],
        out_specs=vmem(2),
        scratch_shapes=buffers,
        compiler_params=params(),
        name="growth",
    )(arrived, above, amounts)

    parts = lax.all_to_all(part, ("gx", "gy"), 0, 0, tiled=True)

    out = pl.pallas_call(
        final_kernel,
        out_shape=shaped((slots, tracers, width), f32),
        in_specs=vmem(4) + [any_hbm],
        out_specs=any_hbm,
        scratch_shapes=[
            buffers[0],
            pltpu.VMEM((group * tracers, group * tracers), bf16),
            pltpu.VMEM((width // LANES, group, LANES), f32),
            pltpu.VMEM((group * tracers, width), f32),
            pltpu.VMEM((width // LANES, group, tracers, LANES), f32),
            buffers[1],
            pltpu.SemaphoreType.DMA((steps,)),
        ],
        compiler_params=params(),
        name="final",
    )(parts, arrived, weight, reaction_rates, amounts)

    thermal_final = pl.pallas_call(
        functools.partial(warm_kernel, bx_n, by_n, n_gy),
        out_shape=shaped((levels, nx, ny), f32),
        in_specs=vmem(5 + n_gy),
        out_specs=pl.BlockSpec(memory_space=pltpu.VMEM),
        scratch_shapes=[pltpu.VMEM((n_blocks, width), f32)],
        compiler_params=params(),
        name="warm",
    )(sel_t, light, flags, tally, stepped, *returned)
    return thermal_final, out.reshape(solute_amounts.shape)


def solution(mesh):
    return jax.shard_map(
        on_device,
        mesh=mesh,
        in_specs=(
            P(None, "gx", "gy"),
            P("gx", "gy"),
            P("gx", "gy"),
            P("gx", "gy", None),
            P("gx", "gy", None),
            P("gx", "gy", None, None),
            P("gx", "gy", None, None, None),
            P(),
        ),
        out_specs=(P(None, "gx", "gy"), P("gx", "gy", None, None, None)),
        check_vma=False,
    )
```

time: 187 us -> 78.1 us (0.42)
  other arithmetic: 43 us -> 0 us
  blocking collectives: 40.8 us -> 0 us
  local copies, waits for them, and re-layouts: 37.5 us -> 0.02 us
  Pallas kernels: 0 us -> 25.5 us
  matrix products: 24.1 us -> 0 us
  waiting for transfers between devices: 12.9 us -> 21 us
  starting transfers between devices: 26.1 us -> 29.9 us
    psum x1 -> x0, blocking collectives: 40.8 us -> none  [on_device(): old_total, cells = lax.psum((old_local, cells_local), ('gx', 'gy'))]
    pallas_call x0 -> x7, Pallas kernels: none -> 25.5 us  [the longest x1 9.51 us: on_device(): pl.pallas_call(final_kernel, out_shape=shaped((slots, tracers, width), f3...]
    dot_general x3 -> x0, matrix products: 24.1 us -> none  [the longest x1 21.6 us: column_step(): jnp.einsum('rs,nsf->nrf', reaction_rates, amounts_on_chip, precision=lax....]
    slice x13 -> x0, local copies, waits for them, and re-layouts: 16 us -> none  [the longest x4 13 us: level_below(): return jnp.concatenate([values[..., 64:], values[..., -64:]], axis=-1)]
    ppermute x4 -> x11, starting transfers between devices: 8.72 us -> 21.5 us  [the longest x7 12.3 us: on_device(): returned.append(lax.ppermute(passed[d], 'gy', pairs))]
    mul x2 -> x0, other arithmetic: 11.8 us -> none  [the longest x1 11.1 us: column_step(): (kappa_flat.astype(jnp.float32) * active)[:, None]]
    reshape x1 -> x0, other arithmetic: 9.28 us -> none  [on_device(): solute_final = jnp.where(valid[:, None] > 0, new + shift[None, :, None],...]
    all_to_all x3 -> x2, starting transfers between devices: 17.3 us -> 8.46 us  [the longest x1 5.75 us: exchange(): y = lax.all_to_all(x.reshape(n_gy, cap, x.shape[1]), 'gy', 0, 0, tiled=True)]
  transfers between devices with their start and end apart: 7 -> 13, of which waited for: 1 -> 5; matrix products, arithmetic and copies ran while one was open for 48% -> 0% of each run, Pallas kernels for 0% -> 9%
where the time goes in v1:
time: 78.1 us; the launch traced here: 77.2 us
  starting transfers between devices  29.9 us (38%)
  Pallas kernels  25.5 us (33%)
  waiting for transfers between devices  21 us (27%)
    all_to_all x1, waiting for transfers between devices, exchange(): y = lax.all_to_all(x.reshape(n_gy, cap, x.shape[1]), 'gy', 0, 0, tiled=True)  13.3 us
    ppermute x7, starting transfers between devices, on_device(): returned.append(lax.ppermute(passed[d], 'gy', pairs))  12.3 us
    pallas_call x1, Pallas kernels, on_device(): pl.pallas_call(final_kernel, out_shape=shaped((slots, tracers, width), f3...  9.51 us
    ppermute x4, starting transfers between devices, onward(): lax.ppermute(x, axis, pairs if way > 0 else [(j, i) for i, j in pairs])  9.2 us
    all_to_all x1, starting transfers between devices, exchange(): y = lax.all_to_all(x.reshape(n_gy, cap, x.shape[1]), 'gy', 0, 0, tiled=True)  5.75 us
    pallas_call x1, Pallas kernels, on_device(): pl.pallas_call(growth_kernel, out_shape=[shaped((width // LANES, slots, L...  4.35 us
    ppermute x7, waiting for transfers between devices, on_device(): returned.append(lax.ppermute(passed[d], 'gy', pairs))  3.9 us
    ppermute x4, waiting for transfers between devices, onward(): lax.ppermute(x, axis, pairs if way > 0 else [(j, i) for i, j in pairs])  3.81 us
  transfers between devices with their start and end apart: 13, of which 5 were waited for; matrix products, arithmetic and copies ran while one was open for 0% of the time, Pallas kernels for 9%

profile of v1, /device:TPU:0, one launch (start us, length us, event | category | flops | bytes accessed | tf_op | source)
XLA Modules:
  0.0 77.2 jit_solution(6925315215169462685)
XLA Ops:
  0.6 1.5 %edges.1 = (f32[40,128]{1,0:T(8,128)S(1)}, f32[40,128]{1,0:T(8,128)S(1)}, f32[16,128]{1,0:T(8,128)S(1)}, f32[16,128]{1,0:T(8,128)S(1)}, f32[32,32,128]{2,1,0:T(8...) custom-call(f32[32,32,128]{2,1,0:T(8,128)} %refs_0_.1, ...), custom_call_target="tpu_custom_call" | custom-call | tf_op jit(solution)/shard_map/edges/pallas_call | solution.py:424
  2.1 2.4 %collective-permute-start = (f32[40,128]{1,0:T(8,128)S(1)}, f32[40,128]{1,0:T(8,128)S(1)}, u32[]{:S(2)}, u32[]{:S(2)}) collective-permute-start(f32[40,128]{1,0:T(8,128)S(1)} %get-tuple-element.35), channel_id=1, source_target_pairs={{0,8},{8,16},{16,24},{1,9},{9,17},{17,25},{2,10},{10,18},{18,26},{... | collective-permute-start | bytes 61448 | tf_op jit(solution)/shard_map/ppermute | solution.py:440
  4.5 1.3 %collective-permute-start.1 = (f32[40,128]{1,0:T(8,128)S(1)}, f32[40,128]{1,0:T(8,128)S(1)}, u32[]{:S(2)}, u32[]{:S(2)}) collective-permute-start(f32[40,128]{1,0:T(8,128)S(1)} %get-tuple-element.36), channel_id=1, source_target_pairs={{8,0},{16,8},{24,16},{9,1},{17,9},{25,17},{10,2},{18,10},{26,18},{... | collective-permute-start | bytes 61448 | tf_op jit(solution)/shard_map/ppermute | solution.py:440
  5.8 4.2 %collective-permute-start.2 = (f32[16,128]{1,0:T(8,128)S(1)}, f32[16,128]{1,0:T(8,128)S(1)}, u32[]{:S(2)}, u32[]{:S(2)}) collective-permute-start(f32[16,128]{1,0:T(8,128)S(1)} %get-tuple-element.37.own_hi), channel_id=1, source_target_pairs={{0,1},{1,2},{2,3},{3,4},{4,5},{5,6},{6,7},{8,9},{9,10},{10,11},{11... | collective-permute-start | bytes 24584 | tf_op jit(solution)/shard_map/ppermute | solution.py:440
  10.0 1.3 %collective-permute-start.3 = (f32[16,128]{1,0:T(8,128)S(1)}, f32[16,128]{1,0:T(8,128)S(1)}, u32[]{:S(2)}, u32[]{:S(2)}) collective-permute-start(f32[16,128]{1,0:T(8,128)S(1)} %get-tuple-element.38.own_lo), channel_id=1, source_target_pairs={{1,0},{2,1},{3,2},{4,3},{5,4},{6,5},{7,6},{9,8},{10,9},{11,10},{12... | collective-permute-start | bytes 24584 | tf_op jit(solution)/shard_map/ppermute | solution.py:440
  11.3 0.4 slots.1
  11.8 0.0 collective-permute-done.2.fylo
  11.8 3.8 %collective-permute-done.3.fyhi = f32[16,128]{1,0:T(8,128)S(1)} collective-permute-done((f32[16,128]{1,0:T(8,128)S(1)}, f32[16,128]{1,0:T(8,128)S(1)}, u32[]{:S(2)}, u32[]{:S(2)}) %collective-permute-start.3) | collective-permute-done | bytes 8224 | tf_op jit(solution)/shard_map/ppermute | solution.py:440
  15.6 0.0 collective-permute-done.fxlo
  15.6 0.0 collective-permute-done.1.fxhi
  15.6 3.2 %stencil.1 = (f32[32,32,128]{2,1,0:T(8,128)S(1)}, bf16[128,2304]{1,0:T(8,128)(2,1)}) custom-call(f32[32,32,128]{2,1,0:T(8,128)S(1)} %get-tuple-element.34.t, s32[1,64]{1,0:T(1,128)S(1)} %get-tuple-element.30.flags, s32[1,64]{1,0:T(1,128)S(1)} %get-tuple-element.31.tally, f32[40,128]{1,0:T(8,128)S(1)} %collective-permute-done.fxlo, ...), custom_call_target="tpu_custom_call" | custom-call | tf_op jit(solution)/shard_map/stencil/pallas_call | solution.py:480
  18.8 5.8 %all-to-all-start = ((bf16[8,16,2304]{2,1,0:T(8,128)(2,1)}), bf16[8,16,2304]{2,1,0:T(8,128)(2,1)S(1)}, u32[]{:S(2)}, u32[]{:S(2)}) async-start(bf16[8,16,2304]{2,1,0:T(8,128)(2,1)} %bitcast.4), calls=%async_computation | async-start | bytes 1179648 | tf_op jit(solution)/shard_map/all_to_all | solution.py:491
  24.6 0.0 copy-start
  24.6 3.8 %clear.1 = (f32[128,2048]{1,0:T(8,128)S(1)}, bf16[16,2048]{1,0:T(8,128)(2,1)S(1)}, bf16[16,2048]{1,0:T(8,128)(2,1)S(1)}, bf16[16,2048]{1,0:T(8,128)(2,1)S(1)}, b...) custom-call(f32[128,8,2048]{2,1,0:T(8,128)} %bitcast.9), custom_call_target="tpu_custom_call" | custom-call | tf_op jit(solution)/shard_map/clear/pallas_call | solution.py:467
  28.4 0.0 copy-start.1
  28.4 0.0 copy-start.2
  28.4 0.0 copy-start.3
  28.4 0.0 copy-start.4
  28.4 13.3 %all-to-all-done = bf16[8,16,2304]{2,1,0:T(8,128)(2,1)S(1)} async-done(((bf16[8,16,2304]{2,1,0:T(8,128)(2,1)}), bf16[8,16,2304]{2,1,0:T(8,128)(2,1)S(1)}, u32[]{:S(2)}, u32[]{:S(2)}) %all-to-all-start) | async-done | bytes 589856 | tf_op jit(solution)/shard_map/all_to_all | solution.py:491
  41.7 0.0 copy-done.1
  41.7 0.0 copy-done.2
  41.7 0.0 copy-done.3
  41.7 0.0 copy-done.4
  41.7 4.3 %growth.1 = (f32[16,128,128]{2,1,0:T(8,128)S(1)}, f32[32,8,128]{2,1,0:T(8,128)}) custom-call(bf16[128,2304]{1,0:T(8,128)(2,1)S(1)} %bitcast.7, f32[128,2048]{1,0:T(8,128)S(1)} %get-tuple-element.51.above, f32[128,8,2048]{2,1,0:T(8,128)} %bitcast.10), custom_call_target="tpu_custom_call" | custom-call | tf_op jit(solution)/shard_map/growth/pallas_call | solution.py:500
  46.1 2.7 %all-to-all-start.1 = ((f32[32,8,128]{2,1,0:T(8,128)}), f32[32,8,128]{2,1,0:T(8,128)S(1)}, u32[]{:S(2)}, u32[]{:S(2)}) async-start(f32[32,8,128]{2,1,0:T(8,128)} %get-tuple-element.52), calls=%async_computation.1 | async-start | bytes 262144 | tf_op jit(solution)/shard_map/all_to_all | solution.py:513
  48.8 1.8 %collective-permute-start.4 = (bf16[16,2048]{1,0:T(8,128)(2,1)}, bf16[16,2048]{1,0:T(8,128)(2,1)S(1)}, u32[]{:S(2)}, u32[]{:S(2)}) collective-permute-start(bf16[16,2048]{1,0:T(8,128)(2,1)} %copy-done.4), channel_id=1, source_target_pairs={{0,1},{1,2},{2,3},{3,4},{4,5},{5,6},{6,7},{7,0},{8,9},{9,10},{10,1... | collective-permute-start | bytes 196616 | tf_op jit(solution)/shard_map/ppermute | solution.py:498
  50.6 1.5 %collective-permute-start.5 = (bf16[16,2048]{1,0:T(8,128)(2,1)}, bf16[16,2048]{1,0:T(8,128)(2,1)S(1)}, u32[]{:S(2)}, u32[]{:S(2)}) collective-permute-start(bf16[16,2048]{1,0:T(8,128)(2,1)} %copy-done.3), channel_id=1, source_target_pairs={{0,2},{1,3},{2,4},{3,5},{4,6},{5,7},{6,0},{7,1},{8,10},{9,11},{10,... | collective-permute-start | bytes 196616 | tf_op jit(solution)/shard_map/ppermute | solution.py:498
  52.1 2.4 %collective-permute-start.6 = (bf16[16,2048]{1,0:T(8,128)(2,1)}, bf16[16,2048]{1,0:T(8,128)(2,1)S(1)}, u32[]{:S(2)}, u32[]{:S(2)}) collective-permute-start(bf16[16,2048]{1,0:T(8,128)(2,1)} %copy-done.2), channel_id=1, source_target_pairs={{0,3},{1,4},{2,5},{3,6},{4,7},{5,0},{6,1},{7,2},{8,11},{9,12},{10,... | collective-permute-start | bytes 196616 | tf_op jit(solution)/shard_map/ppermute | solution.py:498
  54.5 1.4 %collective-permute-start.7 = (bf16[16,2048]{1,0:T(8,128)(2,1)}, bf16[16,2048]{1,0:T(8,128)(2,1)S(1)}, u32[]{:S(2)}, u32[]{:S(2)}) collective-permute-start(bf16[16,2048]{1,0:T(8,128)(2,1)} %copy-done.1), channel_id=1, source_target_pairs={{0,4},{1,5},{2,6},{3,7},{4,0},{5,1},{6,2},{7,3},{8,12},{9,13},{10,... | collective-permute-start | bytes 196616 | tf_op jit(solution)/shard_map/ppermute | solution.py:498
  55.9 2.4 %collective-permute-start.8 = (bf16[16,2048]{1,0:T(8,128)(2,1)S(1)}, bf16[16,2048]{1,0:T(8,128)(2,1)S(1)}, u32[]{:S(2)}, u32[]{:S(2)}) collective-permute-start(bf16[16,2048]{1,0:T(8,128)(2,1)S(1)} %get-tuple-element.47), channel_id=1, source_target_pairs={{0,5},{1,6},{2,7},{3,0},{4,1},{5,2},{6,3},{7,4},{8,13},{9,14},{10,... | collective-permute-start | bytes 196616 | tf_op jit(solution)/shard_map/ppermute | solution.py:498
  58.3 0.1 collective-permute-done.4.rest_1_
  58.5 1.3 %collective-permute-start.9 = (bf16[16,2048]{1,0:T(8,128)(2,1)S(1)}, bf16[16,2048]{1,0:T(8,128)(2,1)S(1)}, u32[]{:S(2)}, u32[]{:S(2)}) collective-permute-start(bf16[16,2048]{1,0:T(8,128)(2,1)S(1)} %get-tuple-element.48), channel_id=1, source_target_pairs={{0,6},{1,7},{2,0},{3,1},{4,2},{5,3},{6,4},{7,5},{8,14},{9,15},{10,... | collective-permute-start | bytes 196616 | tf_op jit(solution)/shard_map/ppermute | solution.py:498
  59.7 0.0 collective-permute-done.5.rest_2_
  59.8 1.5 %collective-permute-start.10 = (bf16[16,2048]{1,0:T(8,128)(2,1)S(1)}, bf16[16,2048]{1,0:T(8,128)(2,1)S(1)}, u32[]{:S(2)}, u32[]{:S(2)}) collective-permute-start(bf16[16,2048]{1,0:T(8,128)(2,1)S(1)} %get-tuple-element.49), channel_id=1, source_target_pairs={{0,7},{1,0},{2,1},{3,2},{4,3},{5,4},{6,5},{7,6},{8,15},{9,8},{10,9... | collective-permute-start | bytes 196616 | tf_op jit(solution)/shard_map/ppermute | solution.py:498
  61.2 2.4 %collective-permute-done.6.rest_3_ = bf16[16,2048]{1,0:T(8,128)(2,1)S(1)} collective-permute-done((bf16[16,2048]{1,0:T(8,128)(2,1)}, bf16[16,2048]{1,0:T(8,128)(2,1)S(1)}, u32[]{:S(2)}, u32[]{:S(2)}) %collective-permute-start.6) | collective-permute-done | bytes 65568 | tf_op jit(solution)/shard_map/ppermute | solution.py:498
  63.6 0.0 collective-permute-done.7.rest_4_
  63.6 0.0 collective-permute-done.8.rest_5_
  63.6 1.3 %collective-permute-done.9.rest_6_ = bf16[16,2048]{1,0:T(8,128)(2,1)S(1)} collective-permute-done((bf16[16,2048]{1,0:T(8,128)(2,1)S(1)}, bf16[16,2048]{1,0:T(8,128)(2,1)S(1)}, u32[]{:S(2)}, u32[]{:S(2)}) %collective-permute-start.9) | collective-permute-done | bytes 65568 | tf_op jit(solution)/shard_map/ppermute | solution.py:498
  65.0 0.0 collective-permute-done.10.rest_7_
  65.0 2.7 %warm.1 = f32[32,32,128]{2,1,0:T(8,128)} custom-call(bf16[64,128]{1,0:T(8,128)(2,1)S(1)} %get-tuple-element.33.sel_t, bf16[32,128]{1,0:T(8,128)(2,1)S(1)} %get-tuple-element.29.light, s32[1,64]{1,0:T(1,128)S(1)} %get-tuple-element.30.flags, s32[1,64]{1,0:T(1,128)S(1)} %get-tuple-element.31.tally, f32[32,32,128]{2,1,0:T(8,128)S(1)} %get-tuple-element.41.stepped, ...), custom_call_target="tpu_custom_call" | custom-call | tf_op jit(solution)/shard_map/warm/pallas_call | solution.py:533
  67.7 0.0 all-to-all-done.1.parts
  67.7 0.0 copy-done
  67.7 9.5 %final.1 = f32[128,8,2048]{2,1,0:T(8,128)} custom-call(f32[32,8,128]{2,1,0:T(8,128)S(1)} %all-to-all-done.1.parts, bf16[128,2304]{1,0:T(8,128)(2,1)S(1)} %bitcast.8, f32[16,128,128]{2,1,0:T(8,128)S(1)} %get-tuple-element.53.weight, f32[8,8]{1,0:T(8,128)S(1)} %copy-done, f32[128,8,2048]{2,1,0:T(8,128)} %bitcast.11), custom_call_target="tpu_custom_call" | custom-call | tf_op jit(solution)/shard_map/final/pallas_call | solution.py:515
Async XLA Ops:
  2.1 13.5 %collective-permute-start = (f32[40,128]{1,0:T(8,128)S(1)}, f32[40,128]{1,0:T(8,128)S(1)}, u32[]{:S(2)}, u32[]{:S(2)}) collective-permute-start(f32[40,128]{1,0:T(8,128)S(1)} %get-tuple-element.35), channel_id=1, source_target_pairs={{0,8},{8,16},{16,24},{1,9},{9,17},{17,25},{2,10},{10,18},{18,26},{... | collective-permute-start | bytes 61448 | tf_op jit(solution)/shard_map/ppermute | solution.py:440
  4.5 11.1 %collective-permute-start.1 = (f32[40,128]{1,0:T(8,128)S(1)}, f32[40,128]{1,0:T(8,128)S(1)}, u32[]{:S(2)}, u32[]{:S(2)}) collective-permute-start(f32[40,128]{1,0:T(8,128)S(1)} %get-tuple-element.36), channel_id=1, source_target_pairs={{8,0},{16,8},{24,16},{9,1},{17,9},{25,17},{10,2},{18,10},{26,18},{... | collective-permute-start | bytes 61448 | tf_op jit(solution)/shard_map/ppermute | solution.py:440
  5.8 6.0 %collective-permute-start.2 = (f32[16,128]{1,0:T(8,128)S(1)}, f32[16,128]{1,0:T(8,128)S(1)}, u32[]{:S(2)}, u32[]{:S(2)}) collective-permute-start(f32[16,128]{1,0:T(8,128)S(1)} %get-tuple-element.37.own_hi), channel_id=1, source_target_pairs={{0,1},{1,2},{2,3},{3,4},{4,5},{5,6},{6,7},{8,9},{9,10},{10,11},{11... | collective-permute-start | bytes 24584 | tf_op jit(solution)/shard_map/ppermute | solution.py:440
  10.0 5.5 %collective-permute-start.3 = (f32[16,128]{1,0:T(8,128)S(1)}, f32[16,128]{1,0:T(8,128)S(1)}, u32[]{:S(2)}, u32[]{:S(2)}) collective-permute-start(f32[16,128]{1,0:T(8,128)S(1)} %get-tuple-element.38.own_lo), channel_id=1, source_target_pairs={{1,0},{2,1},{3,2},{4,3},{5,4},{6,5},{7,6},{9,8},{10,9},{11,10},{12... | collective-permute-start | bytes 24584 | tf_op jit(solution)/shard_map/ppermute | solution.py:440
  18.8 22.9 %all-to-all-start = ((bf16[8,16,2304]{2,1,0:T(8,128)(2,1)}), bf16[8,16,2304]{2,1,0:T(8,128)(2,1)S(1)}, u32[]{:S(2)}, u32[]{:S(2)}) async-start(bf16[8,16,2304]{2,1,0:T(8,128)(2,1)} %bitcast.4), calls=%async_computation | async-start | bytes 1179648 | tf_op jit(solution)/shard_map/all_to_all | solution.py:491
  24.6 43.1 %copy-start = (f32[8,8]{1,0:T(8,128)S(1)}, f32[8,8]{1,0:T(8,128)}, u32[]{:S(2)}) copy-start(f32[8,8]{1,0:T(8,128)} %rates.1) | copy-start | bytes 772
  28.4 13.3 %copy-start.1 = (bf16[16,2048]{1,0:T(8,128)(2,1)}, bf16[16,2048]{1,0:T(8,128)(2,1)S(1)}, u32[]{:S(2)}) copy-start(bf16[16,2048]{1,0:T(8,128)(2,1)S(1)} %get-tuple-element.46) | copy-start | bytes 196612
  28.4 13.3 %copy-start.2 = (bf16[16,2048]{1,0:T(8,128)(2,1)}, bf16[16,2048]{1,0:T(8,128)(2,1)S(1)}, u32[]{:S(2)}) copy-start(bf16[16,2048]{1,0:T(8,128)(2,1)S(1)} %get-tuple-element.45) | copy-start | bytes 196612
  28.4 13.3 %copy-start.3 = (bf16[16,2048]{1,0:T(8,128)(2,1)}, bf16[16,2048]{1,0:T(8,128)(2,1)S(1)}, u32[]{:S(2)}) copy-start(bf16[16,2048]{1,0:T(8,128)(2,1)S(1)} %get-tuple-element.44) | copy-start | bytes 196612
  28.4 13.3 %copy-start.4 = (bf16[16,2048]{1,0:T(8,128)(2,1)}, bf16[16,2048]{1,0:T(8,128)(2,1)S(1)}, u32[]{:S(2)}) copy-start(bf16[16,2048]{1,0:T(8,128)(2,1)S(1)} %get-tuple-element.43) | copy-start | bytes 196612
  46.1 21.6 %all-to-all-start.1 = ((f32[32,8,128]{2,1,0:T(8,128)}), f32[32,8,128]{2,1,0:T(8,128)S(1)}, u32[]{:S(2)}, u32[]{:S(2)}) async-start(f32[32,8,128]{2,1,0:T(8,128)} %get-tuple-element.52), calls=%async_computation.1 | async-start | bytes 262144 | tf_op jit(solution)/shard_map/all_to_all | solution.py:513
  48.8 9.7 %collective-permute-start.4 = (bf16[16,2048]{1,0:T(8,128)(2,1)}, bf16[16,2048]{1,0:T(8,128)(2,1)S(1)}, u32[]{:S(2)}, u32[]{:S(2)}) collective-permute-start(bf16[16,2048]{1,0:T(8,128)(2,1)} %copy-done.4), channel_id=1, source_target_pairs={{0,1},{1,2},{2,3},{3,4},{4,5},{5,6},{6,7},{7,0},{8,9},{9,10},{10,1... | collective-permute-start | bytes 196616 | tf_op jit(solution)/shard_map/ppermute | solution.py:498
  50.6 9.1 %collective-permute-start.5 = (bf16[16,2048]{1,0:T(8,128)(2,1)}, bf16[16,2048]{1,0:T(8,128)(2,1)S(1)}, u32[]{:S(2)}, u32[]{:S(2)}) collective-permute-start(bf16[16,2048]{1,0:T(8,128)(2,1)} %copy-done.3), channel_id=1, source_target_pairs={{0,2},{1,3},{2,4},{3,5},{4,6},{5,7},{6,0},{7,1},{8,10},{9,11},{10,... | collective-permute-start | bytes 196616 | tf_op jit(solution)/shard_map/ppermute | solution.py:498
  52.1 11.5 %collective-permute-start.6 = (bf16[16,2048]{1,0:T(8,128)(2,1)}, bf16[16,2048]{1,0:T(8,128)(2,1)S(1)}, u32[]{:S(2)}, u32[]{:S(2)}) collective-permute-start(bf16[16,2048]{1,0:T(8,128)(2,1)} %copy-done.2), channel_id=1, source_target_pairs={{0,3},{1,4},{2,5},{3,6},{4,7},{5,0},{6,1},{7,2},{8,11},{9,12},{10,... | collective-permute-start | bytes 196616 | tf_op jit(solution)/shard_map/ppermute | solution.py:498
  54.5 9.1 %collective-permute-start.7 = (bf16[16,2048]{1,0:T(8,128)(2,1)}, bf16[16,2048]{1,0:T(8,128)(2,1)S(1)}, u32[]{:S(2)}, u32[]{:S(2)}) collective-permute-start(bf16[16,2048]{1,0:T(8,128)(2,1)} %copy-done.1), channel_id=1, source_target_pairs={{0,4},{1,5},{2,6},{3,7},{4,0},{5,1},{6,2},{7,3},{8,12},{9,13},{10,... | collective-permute-start | bytes 196616 | tf_op jit(solution)/shard_map/ppermute | solution.py:498
  55.9 7.7 %collective-permute-start.8 = (bf16[16,2048]{1,0:T(8,128)(2,1)S(1)}, bf16[16,2048]{1,0:T(8,128)(2,1)S(1)}, u32[]{:S(2)}, u32[]{:S(2)}) collective-permute-start(bf16[16,2048]{1,0:T(8,128)(2,1)S(1)} %get-tuple-element.47), channel_id=1, source_target_pairs={{0,5},{1,6},{2,7},{3,0},{4,1},{5,2},{6,3},{7,4},{8,13},{9,14},{10,... | collective-permute-start | bytes 196616 | tf_op jit(solution)/shard_map/ppermute | solution.py:498
  58.5 6.5 %collective-permute-start.9 = (bf16[16,2048]{1,0:T(8,128)(2,1)S(1)}, bf16[16,2048]{1,0:T(8,128)(2,1)S(1)}, u32[]{:S(2)}, u32[]{:S(2)}) collective-permute-start(bf16[16,2048]{1,0:T(8,128)(2,1)S(1)} %get-tuple-element.48), channel_id=1, source_target_pairs={{0,6},{1,7},{2,0},{3,1},{4,2},{5,3},{6,4},{7,5},{8,14},{9,15},{10,... | collective-permute-start | bytes 196616 | tf_op jit(solution)/shard_map/ppermute | solution.py:498
  59.8 5.2 %collective-permute-start.10 = (bf16[16,2048]{1,0:T(8,128)(2,1)S(1)}, bf16[16,2048]{1,0:T(8,128)(2,1)S(1)}, u32[]{:S(2)}, u32[]{:S(2)}) collective-permute-start(bf16[16,2048]{1,0:T(8,128)(2,1)S(1)} %get-tuple-element.49), channel_id=1, source_target_pairs={{0,7},{1,0},{2,1},{3,2},{4,3},{5,4},{6,5},{7,6},{8,15},{9,8},{10,9... | collective-permute-start | bytes 196616 | tf_op jit(solution)/shard_map/ppermute | solution.py:498

commit v2 on v1

v2 whole, which is shorter than its diff:
```python
import functools
import jax
import jax.numpy as jnp
from jax import lax
from jax.experimental import pallas as pl
from jax.experimental.pallas import tpu as pltpu
from jax.sharding import PartitionSpec as P

NU_COEF = 0.2
STEP_DT = 0.05
ATTEN_WATER = 0.06
ATTEN_CHL = 0.05
WARMING_SCALE = 0.5
GROWTH_TEMP = 0.063
LANES = 128
HALF = 64
SUB = 8
AHEAD = 4
DEEP = 3
BATCH = 16
WARM_BATCH = 16


f32 = jnp.float32
bf16 = jnp.bfloat16


def iota(shape, dim):
    return lax.broadcasted_iota(jnp.int32, shape, dim)


def swap_granules(x):
    row = iota(x.shape, 1)
    lane = iota(x.shape, 2)
    for step in (1, 2, 4):
        r = (row & step) != 0
        c = (lane & (step * SUB)) != 0
        w = step * SUB
        up = pltpu.roll(pltpu.roll(x, SUB - step, 1), w, 2)
        down = pltpu.roll(pltpu.roll(x, step, 1), LANES - w, 2)
        x = jnp.where(r == c, x, jnp.where(c, up, down))
    return x


def join_levels(a, b):
    low = iota(a.shape, 2) < HALF
    return (
        jnp.where(low, a, pltpu.roll(b, HALF, 2)),
        jnp.where(low, pltpu.roll(a, HALF, 2), b),
    )


def row_of(ref, *at, n=SUB):
    return ref[(*at[:-1], pl.ds(at[-1], n, stride=0), slice(None))]


def depth_rows(depth, blocks_y):
    n = depth.shape[1]
    mine = iota((SUB, n), 1) // blocks_y == iota((SUB, n), 0)
    left = jnp.where(mine, jnp.broadcast_to(depth, (SUB, n)), 0.0)
    spread = iota((n, LANES), 0) % blocks_y == iota((n, LANES), 1) // SUB
    return jnp.dot(left, spread.astype(f32), preferred_element_type=f32)


def edge_depth(depth, blocks_x, blocks_y, by):
    n = depth.shape[1]
    pick = iota((n, LANES), 0) == (iota((n, LANES), 1) % blocks_x) * blocks_y + by
    return jnp.dot(
        jnp.broadcast_to(depth, (SUB, n)), pick.astype(f32), preferred_element_type=f32
    )


def edges_kernel(bx_n, by_n, *refs):
    sources, (x1, x2, y1, y2), held, sems = refs[:6], refs[6:10], refs[10:16], refs[16]
    even_x = lax.axis_index("gx") % 2 == 0
    even_y = lax.axis_index("gy") % 2 == 0
    t, flags, tally = held[:3]
    levels, nx, _ = t.shape
    loads = [
        pltpu.make_async_copy(x, y, sems.at[i]) for i, (x, y) in enumerate(zip(sources, held))
    ]
    for load in loads:
        load.start()
    for load in loads:
        load.wait()
    depth = (flags[...] * tally[...]).astype(f32)
    d = depth_rows(depth, by_n)
    for k in range(levels):
        first, last = t[k, 0:1, :], t[k, nx - 1 : nx, :]
        x1[k : k + 1, :] = jnp.where(even_x, last, first)
        x2[k : k + 1, :] = jnp.where(even_x, first, last)
    first = jnp.broadcast_to(d[0:1], (SUB, LANES))
    last = jnp.broadcast_to(d[bx_n - 1 : bx_n], (SUB, LANES))
    x1[levels : levels + SUB, :] = jnp.where(even_x, last, first)
    x2[levels : levels + SUB, :] = jnp.where(even_x, first, last)
    lane = iota((SUB, LANES), 1)
    lo = jnp.zeros((SUB, LANES), f32)
    hi = jnp.zeros((SUB, LANES), f32)
    for k0 in range(0, levels, 4):
        places = [(k, bx) for k in range(k0, k0 + 4) for bx in range(bx_n)]
        tiles = [t[k, bx * SUB : (bx + 1) * SUB, :] for k, bx in places]
        js = [k * bx_n + bx for k, bx in places]
        los = [pltpu.roll(v, j, 1) for v, j in zip(tiles, js)]
        his = [pltpu.roll(v, (j + 1) % LANES, 1) for v, j in zip(tiles, js)]
        for j, a, b in zip(js, los, his):
            lo = jnp.where(lane == j, a, lo)
            hi = jnp.where(lane == j, b, hi)
    y1[0:SUB, :] = jnp.where(even_y, hi, lo)
    y2[0:SUB, :] = jnp.where(even_y, lo, hi)
    k_lane = (lane // bx_n).astype(f32)
    in_lo = (k_lane < edge_depth(depth, bx_n, by_n, 0)).astype(f32)
    in_hi = (k_lane < edge_depth(depth, bx_n, by_n, by_n - 1)).astype(f32)
    y1[SUB:, :] = jnp.where(even_y, in_hi, in_lo)
    y2[SUB:, :] = jnp.where(even_y, in_lo, in_hi)


def ranks(holder):
    n = holder.shape[1]
    row_i = iota((n, n), 0)
    col_i = iota((n, n), 1)
    own = holder[...].astype(f32)
    own_row = jnp.broadcast_to(own, (n, n))
    own_col = jnp.sum(jnp.where(row_i == col_i, own_row, 0.0), axis=1, keepdims=True)
    same = own_row == own_col
    rank_row = jnp.sum(jnp.where(same & (row_i < col_i), 1.0, 0.0), axis=0, keepdims=True)
    rank_col = jnp.sum(jnp.where(same & (col_i < row_i), 1.0, 0.0), axis=1, keepdims=True)
    return own, rank_row, own_col, rank_col


def slots_kernel(bx_n, by_n, cap, amb, light, flags, tally, holder, sel, tail):
    n = bx_n * by_n
    slots = sel.shape[0]
    _, rank_row, _, _ = ranks(holder)
    turn = jnp.bitwise_xor(holder[...], lax.axis_index("gy")).astype(f32)
    chosen = (iota((slots, n), 0).astype(f32) == turn * cap + rank_row).astype(bf16)
    sel[...] = chosen
    row_i = iota((n, n), 0)
    col_i = iota((n, n), 1)
    depth = (flags[...] * tally[...]).astype(f32)
    depth_col = jnp.sum(
        jnp.where(row_i == col_i, jnp.broadcast_to(depth, (n, n)), 0.0), axis=1, keepdims=True
    )
    a = amb[...].astype(f32).reshape(bx_n, SUB, LANES)
    b = light[...].astype(f32).reshape(bx_n, SUB, LANES)
    halves = jnp.stack(join_levels(a, b), axis=1).reshape(2 * bx_n, SUB, LANES)
    rows = swap_granules(halves).reshape(n, LANES)
    fields = jnp.concatenate([rows, jnp.broadcast_to(depth_col, (n, LANES))], axis=1).astype(bf16)
    tail[...] = jnp.dot(chosen, fields, preferred_element_type=f32).astype(bf16)


def stencil_kernel(
    bx_n, by_n, t, flags, tally, x1, x2, y1, y2, own_1, own_2, sel, tail, stepped_hbm, *rest
):
    packed, (blocks, fxlo, fxhi, stepped, sems) = rest[:-5], rest[-5:]
    sends = []
    even_x = lax.axis_index("gx") % 2 == 0
    even_y = lax.axis_index("gy") % 2 == 0
    fxlo[...] = jnp.where(even_x, x2[...], x1[...])
    fxhi[...] = jnp.where(even_x, x1[...], x2[...])
    add_1 = y1[SUB:, :] * (y1[0:SUB, :] - own_1[0:SUB, :])
    add_2 = y2[SUB:, :] * (y2[0:SUB, :] - own_2[0:SUB, :])
    add_lo = jnp.where(even_y, add_2, add_1)
    add_hi = jnp.where(even_y, add_1, add_2)
    levels = t.shape[0]
    width = levels * HALF
    depth = (flags[...] * tally[...]).astype(f32)
    d = depth_rows(depth, by_n)
    nx = t.shape[1]
    some = BATCH
    lane = iota((nx, LANES), 1)
    row = iota((nx, LANES), 0)
    d_lo = jnp.broadcast_to(fxlo[levels : levels + 1, :], (nx, LANES))
    d_hi = jnp.broadcast_to(fxhi[levels : levels + 1, :], (nx, LANES))
    d_at = jnp.concatenate(
        [jnp.broadcast_to(d[bx : bx + 1], (SUB, LANES)) for bx in range(bx_n)], axis=0
    )
    d_xm = jnp.where(row == 0, d_lo, pltpu.roll(d_at, 1, 0))[None]
    d_xp = jnp.where(row == nx - 1, d_hi, pltpu.roll(d_at, nx - 1, 0))[None]
    d_ym = jnp.where(lane == 0, 0.0, pltpu.roll(d_at, 1, 1))[None]
    d_yp = jnp.where(lane == LANES - 1, 0.0, pltpu.roll(d_at, LANES - 1, 1))[None]
    d_at = d_at[None]
    row = iota((some, nx, LANES), 1)
    lane = iota((some, nx, LANES), 2)
    for k0 in range(0, levels, some):
        ks = range(k0, k0 + some)
        kf = (k0 + iota((some, 1, 1), 0)).astype(f32)
        c = t[k0 : k0 + some]
        xm = pltpu.roll(c, 1, 1)
        xp = pltpu.roll(c, nx - 1, 1)
        ym = pltpu.roll(c, 1, 2)
        yp = pltpu.roll(c, LANES - 1, 2)
        edges = []
        for add, to in ((add_lo, 0), (add_hi, LANES - 1)):
            js = range(k0 * bx_n, (k0 + some) * bx_n)
            rolled = [pltpu.roll(add, (to - j) % LANES, 1) for j in js]
            edges.append(jnp.concatenate(rolled, axis=0).reshape(some, nx, LANES))
        xm = jnp.where(row == 0, jnp.stack([row_of(fxlo, k, n=nx) for k in ks]), xm)
        xp = jnp.where(row == nx - 1, jnp.stack([row_of(fxhi, k, n=nx) for k in ks]), xp)
        total = jnp.where(d_xm > kf, xm - c, 0.0)
        total = total + jnp.where(d_xp > kf, xp - c, 0.0)
        total = total + jnp.where(lane == 0, edges[0], jnp.where(d_ym > kf, ym - c, 0.0))
        total = total + jnp.where(lane == LANES - 1, edges[1], jnp.where(d_yp > kf, yp - c, 0.0))
        s = c + jnp.where(d_at > kf, NU_COEF * total, 0.0)
        stepped[k0 : k0 + some] = s
        rows = pl.ds(k0, some)
        sends.append(
            pltpu.make_async_copy(stepped.at[rows], stepped_hbm.at[rows], sems.at[len(sends)])
        )
        sends[-1].start()
        done = s.reshape(some, bx_n, SUB, LANES)
        halves = []
        for p in range(0, some, 2):
            halves += list(join_levels(done[p], done[p + 1]))
        out = swap_granules(jnp.concatenate(halves, axis=0))
        for q in range(some):
            kp = k0 // 2 + q // 2
            for bx in range(bx_n):
                g = (bx * 2 + q % 2) * SUB
                blocks[g : g + SUB, kp * LANES : (kp + 1) * LANES] = out[q * bx_n + bx]
    chosen = jnp.dot(sel[...], blocks[...].astype(bf16), preferred_element_type=f32).astype(bf16)
    cap = packed[0].shape[0]
    for i, chunk in enumerate(packed):
        chunk[:, :width] = chosen[i * cap : (i + 1) * cap]
        chunk[:, width:] = tail[i * cap : (i + 1) * cap]
    for send in sends:
        send.wait()


def clear_kernel(n_gy, c, above, buf, *rest):
    sent, (passed, sems, out_sems) = rest[:n_gy], rest[n_gy:]
    cap = passed.shape[1]
    width = above.shape[1]
    me = lax.axis_index("gy")
    chunks = [jnp.bitwise_xor(me, i) * cap for i in range(n_gy)]
    loads = [
        pltpu.make_async_copy(c.at[pl.ds(r, cap)], buf.at[i], sems.at[i])
        for i, r in enumerate(chunks)
    ]
    sends = [pltpu.make_async_copy(passed.at[i], sent[i], out_sems.at[i]) for i in range(n_gy)]
    for load in loads:
        load.start()
    low = iota((cap, LANES), 1) < HALF
    spans = [slice(v * LANES, (v + 1) * LANES) for v in range(width // LANES)]
    for i in range(n_gy):
        loads[i].wait()
        a = [ATTEN_WATER + ATTEN_CHL * buf[i, :, 0, at] for at in spans]
        both = [x + pltpu.roll(x, HALF, 1) for x in a]
        carry = jnp.zeros((cap, LANES), f32)
        sums = []
        for x, y in zip(a, both):
            sums.append(carry + jnp.where(low, x, y))
            carry = carry + y
        left = [jnp.exp(-x) for x in sums]
        before = [jnp.ones((cap, LANES), f32)] + left[:-1]
        prev = [pltpu.roll(jnp.where(low, x, y), HALF, 1) for x, y in zip(left, before)]
        for at, x, y in zip(spans, prev, left):
            above[i * cap : (i + 1) * cap, at] = x
            passed[i, :, at] = (x - y).astype(bf16)
        sends[i].start()
    for send in sends:
        send.wait()


def spread_tail(arrived, rows, width):
    tail = arrived[rows, width : width + LANES].astype(f32)
    count = arrived[rows, width + LANES :].astype(f32)
    low = iota(tail.shape, 1) < HALF
    turned = pltpu.roll(tail, HALF, 1)
    return jnp.where(low, tail, turned), jnp.where(low, turned, tail), count


def growth_kernel(n_gy, above, c, *rest):
    came, (arrived, weight, part) = rest[:n_gy], rest[n_gy:]
    chunks, group, tracers, width = c.shape
    for i, chunk in enumerate(came):
        arrived[i * group : (i + 1) * group, :] = chunk[...]
    spans = [slice(v * LANES, (v + 1) * LANES) for v in range(width // LANES)]
    half = (iota((group, LANES), 1) // HALF).astype(f32)

    def weigh(i):
        rows = pl.ds(pl.multiple_of(i * group, group), group)
        _, light, count = spread_tail(arrived, rows, width)
        tops = [light * above[rows, at] for at in spans]
        temp = [jnp.exp(GROWTH_TEMP * arrived[rows, at].astype(f32)) for at in spans]
        rest = [1.0 / (x + 1.0) for x in tops]
        for v in range(len(spans)):
            g = STEP_DT * (temp[v] * (tops[v] * rest[v]))
            weight[v, rows, :] = jnp.where(half + float(2 * v) < count, g, 0.0)
        return count

    def gather(i, sums):
        r = pl.multiple_of(i * group, group)
        sums = list(sums)
        for v, at in enumerate(spans):
            for s in range(group):
                sums[s % 8] = sums[s % 8] + row_of(weight, v, r + s) * c[i, s, :, at]
        return sums

    def one(i, carry):
        sums = gather(i - 1, carry[:-1])
        return (*sums, carry[-1] + weigh(i))

    start = (*[jnp.zeros((tracers, LANES), f32)] * 8, weigh(0))
    *sums, counts = lax.fori_loop(1, chunks, one, start)
    sums = gather(chunks - 1, sums)
    total = functools.reduce(jnp.add, sums)
    total = total + pltpu.roll(total, HALF, 1)
    wet = jnp.broadcast_to(jnp.sum(counts, axis=0, keepdims=True), (tracers, LANES))
    line = jnp.where(iota((tracers, LANES), 1) < HALF, total, wet)
    part[...] = jnp.broadcast_to(line[None], part.shape)


def mixing_kernel(arrived, mix):
    steps, slots, _ = mix.shape
    width = steps * LANES
    group = 16
    half = (iota((group, LANES), 1) // HALF).astype(f32)
    low = iota((group, LANES), 1) < HALF
    spans = [slice(v * LANES, (v + 1) * LANES) for v in range(steps)]

    def one(i, carry):
        rows = pl.ds(pl.multiple_of(i * group, group), group)
        amb, _, count = spread_tail(arrived, rows, width)
        here = [arrived[rows, at].astype(f32) for at in spans]
        below = [
            pltpu.roll(jnp.where(low, y, x), HALF, 1) for x, y in zip(here, here[1:] + here[-1:])
        ]
        bend = [jnp.tanh(x - y) for x, y in zip(here, below)]
        for v in range(steps):
            m = (amb * (1.0 + 0.5 * bend[v])).astype(bf16).astype(f32)
            mix[v, rows, :] = jnp.where(half + float(2 * v + 1) < count, STEP_DT * m, 0.0)
        return carry

    lax.fori_loop(0, slots // group, one, 0)


def final_kernel(
    cap, parts, arrived, weight, mix, rates_hbm, c, out, done, buf, rates, reactions, mix_up, mixed,
    sems, out_sems, rates_sem,
):
    chunks, group, tracers, width = buf.shape
    me = lax.axis_index("gy")
    rates_load = pltpu.make_async_copy(rates_hbm, rates, rates_sem)
    rates_load.start()

    def load(i):
        at = i * group
        r = jnp.bitwise_xor(me, at // cap) * cap + at % cap
        return c.at[pl.ds(r, group)], buf.at[i], out.at[pl.ds(r, group)]

    def start(i):
        source, kept, _ = load(i)
        pltpu.make_async_copy(source, kept, sems.at[i]).start()

    for i in range(AHEAD):
        start(i)
    rates_load.wait()
    n_rows = group * tracers
    lane = iota((tracers, LANES), 1)
    steps = width // LANES
    spans = [slice(v * LANES, (v + 1) * LANES) for v in range(steps)]

    total = jnp.sum(parts[...], axis=0)
    grown = jnp.sum(jnp.where(lane < HALF, total, 0.0), axis=1, keepdims=True)
    cells = HALF * total[:, LANES - 1 :]
    change = jnp.zeros((tracers, LANES), f32)
    for s in range(tracers):
        change = change + rates[:, s : s + 1] * jnp.broadcast_to(
            grown[s : s + 1, :], (tracers, LANES)
        )
    move = (-change / jnp.maximum(cells, 1.0))[None]
    i_row = iota((n_rows, tracers), 0) % tracers == iota((n_rows, tracers), 1)
    j_col = iota((tracers, n_rows), 1) % tracers == iota((tracers, n_rows), 0)
    spread = jnp.dot(i_row.astype(f32), rates[...], preferred_element_type=f32)
    spread = jnp.dot(spread, j_col.astype(f32), preferred_element_type=f32)
    one_slot = iota((n_rows, n_rows), 0) // tracers == iota((n_rows, n_rows), 1) // tracers
    reactions[...] = jnp.where(one_slot, spread, 0.0).astype(bf16)

    half = (iota((group, LANES), 1) // HALF).astype(f32)
    low = iota((group, LANES), 1) < HALF
    low3 = iota((4, tracers, LANES), 2) < HALF

    def one(i, carry):
        r = pl.multiple_of(i * group, group)
        rows = pl.ds(r, group)

        @pl.when(i + AHEAD < chunks)
        def _():
            start(i + AHEAD)

        source, kept_at, goes = load(i)
        pltpu.make_async_copy(source, kept_at, sems.at[i]).wait()
        count = arrived[rows, width + LANES :].astype(f32)
        kept = [mix[v, rows, :] for v in range(steps)]
        zero = jnp.zeros_like(kept[0])
        for v, (x, y) in enumerate(zip(kept, [zero] + kept[:-1])):
            mix_up[v] = pltpu.roll(jnp.where(low, x, y), HALF, 1)
        mixed[...] = jnp.dot(
            reactions[...], buf[i].reshape(n_rows, width).astype(bf16), preferred_element_type=f32
        )

        spare = count - half
        for s0 in range(0, group, 4):
            some = range(s0, s0 + 4)
            left = jnp.stack(
                [jnp.broadcast_to(spare[s : s + 1, :], (tracers, LANES)) for s in some]
            )
            at_v = lambda v: buf[i, s0 : s0 + 4, :, spans[min(v, steps - 1)]]
            stacked = lambda ref, v, r0: jnp.stack([row_of(ref, v, r0 + s) for s in some])
            turn = lambda x, y: pltpu.roll(jnp.where(low3, y, x), HALF, 2)
            xs = [at_v(v) for v in range(DEEP + 1)]
            turns = [turn(xs[v], xs[v + 1]) for v in range(DEEP)]
            before = pltpu.roll(xs[0], HALF, 2)
            for v, at in enumerate(spans):
                xs.append(at_v(v + DEEP + 1))
                turns.append(turn(xs[DEEP], xs[DEEP + 1]))
                x, z = xs.pop(0), turns.pop(0)
                m = mixed[s0 * tracers : (s0 + 4) * tracers, at].reshape(4, tracers, LANES)
                flux = stacked(mix, v, r) * (z - x) - stacked(mix_up, v, 0) * (x - before)
                y = x + (flux + stacked(weight, v, r) * m)
                buf[i, s0 : s0 + 4, :, at] = y + jnp.where(left > float(2 * v), move, 0.0)
                before = z
        pltpu.make_async_copy(kept_at, goes, out_sems.at[i]).start()
        return carry

    lax.fori_loop(0, chunks, one, 0)
    done[...] = move[0]
    for i in range(chunks):
        _, kept_at, goes = load(i)
        pltpu.make_async_copy(kept_at, goes, out_sems.at[i]).wait()


def warm_kernel(bx_n, by_n, n_gy, holder, light, flags, tally, stepped_hbm, _, *rest):
    returned, (out, blocks, stepped, sem) = rest[:n_gy], rest[n_gy:]
    fetch = pltpu.make_async_copy(stepped_hbm, stepped, sem)
    fetch.start()
    levels, nx, ny = stepped.shape
    cap = returned[0].shape[0]
    n = bx_n * by_n
    _, _, own_col, rank_col = ranks(holder)
    turn = jnp.bitwise_xor(own_col.astype(jnp.int32), lax.axis_index("gy")).astype(f32)
    to_col = turn * cap + rank_col
    sel_t = (iota((n, n_gy * cap), 1).astype(f32) == to_col).astype(bf16)
    got = jnp.concatenate([r[...] for r in returned], axis=0)
    blocks[...] = jnp.dot(sel_t, got, preferred_element_type=f32)
    depth = (flags[...] * tally[...]).astype(f32)
    d = depth_rows(depth, by_n)
    d_at = jnp.concatenate(
        [jnp.broadcast_to(d[bx : bx + 1], (SUB, LANES)) for bx in range(bx_n)], axis=0
    )
    scale = WARMING_SCALE * light[...].astype(f32)
    fetch.wait()
    for k0 in range(0, levels, WARM_BATCH):
        halves = []
        for q in range(WARM_BATCH):
            kp = k0 // 2 + q // 2
            for bx in range(bx_n):
                g = (bx * 2 + q % 2) * SUB
                halves.append(blocks[g : g + SUB, kp * LANES : (kp + 1) * LANES])
        swapped = swap_granules(jnp.stack(halves))
        for p in range(WARM_BATCH // 2):
            lo = swapped[2 * p * bx_n : (2 * p + 1) * bx_n]
            hi = swapped[(2 * p + 1) * bx_n : (2 * p + 2) * bx_n]
            for e, took in enumerate(join_levels(lo, hi)):
                k = k0 + 2 * p + e
                out[k] = stepped[k] + jnp.where(d_at > float(k), scale * took.reshape(nx, ny), 0.0)


def vmem(n):
    return [pl.BlockSpec(memory_space=pltpu.VMEM)] * n


def shaped(shape, dtype):
    return jax.ShapeDtypeStruct(shape, dtype)


def params():
    return pltpu.CompilerParams(vmem_limit_bytes=20 << 20)


def in_hbm(x):
    return pltpu.with_memory_space_constraint(x, pltpu.HBM)


def on_device(
    thermal_anomaly,
    ambient_diffusion,
    solar_light,
    sea_tile_flags,
    flooded_layer_tally,
    tile_holder_rank,
    solute_amounts,
    reaction_rates,
):
    levels, nx, ny = thermal_anomaly.shape
    bx_n, by_n = nx // 8, ny // 8
    n_blocks = bx_n * by_n
    slots, tracers, width = solute_amounts.shape[2:]
    n_gy = lax.axis_size("gy")
    n_all = n_gy * lax.axis_size("gx")
    cap = slots // n_gy
    flags = sea_tile_flags.reshape(1, n_blocks)
    tally = flooded_layer_tally.reshape(1, n_blocks)
    holder = tile_holder_rank.reshape(1, n_blocks)
    amounts = in_hbm(solute_amounts.reshape(slots, tracers, width))

    sources = [thermal_anomaly, flags, tally, ambient_diffusion, solar_light, holder]
    x1, x2, y1, y2, *held = pl.pallas_call(
        functools.partial(edges_kernel, bx_n, by_n),
        out_shape=[shaped((levels + SUB, LANES), f32)] * 2
        + [shaped((2 * SUB, LANES), f32)] * 2
        + [pltpu.VMEM(x.shape, x.dtype) for x in sources],
        in_specs=[pl.BlockSpec(memory_space=pltpu.HBM)] * len(sources),
        out_specs=vmem(4 + len(sources)),
        scratch_shapes=[pltpu.SemaphoreType.DMA((len(sources),))],
        compiler_params=params(),
        name="edges",
    )(*[in_hbm(x) for x in sources])
    thermal, flags, tally, ambient, light, holder = held

    def traded(x, axis, first):
        count = lax.axis_size(axis)
        pairs = [(i, i + 1) for i in range(first, count - 1, 2)]
        return lax.ppermute(x, axis, pairs + [(j, i) for i, j in pairs])

    far_y2 = traded(y2, "gy", 1)
    far_x2 = traded(x2, "gx", 1)
    far_y1 = traded(y1, "gy", 0)
    far_x1 = traded(x1, "gx", 0)

    sel, tail = pl.pallas_call(
        functools.partial(slots_kernel, bx_n, by_n, cap),
        out_shape=[
            shaped((slots, n_blocks), bf16),
            shaped((slots, 2 * LANES), bf16),
        ],
        in_specs=vmem(5),
        out_specs=vmem(2),
        compiler_params=params(),
        name="slots",
    )(ambient, light, flags, tally, holder)

    group = min(16, cap)
    steps = slots // group
    buffers = [
        pltpu.VMEM((steps, group, tracers, width), f32),
        pltpu.SemaphoreType.DMA((steps,)),
    ]
    any_hbm = pl.BlockSpec(memory_space=pltpu.HBM)
    above, held_amounts, *passed = pl.pallas_call(
        functools.partial(clear_kernel, n_gy),
        out_shape=[
            pltpu.VMEM((slots, width), f32),
            pltpu.VMEM((n_gy, cap, tracers, width), f32),
        ]
        + [pltpu.HBM((cap, width), bf16)] * n_gy,
        in_specs=[any_hbm],
        out_specs=vmem(2) + [any_hbm] * n_gy,
        scratch_shapes=[
            pltpu.VMEM((n_gy, cap, width), bf16),
            pltpu.SemaphoreType.DMA((n_gy,)),
            pltpu.SemaphoreType.DMA((n_gy,)),
        ],
        compiler_params=params(),
        name="clear",
    )(amounts)

    stepped, *packed = pl.pallas_call(
        functools.partial(stencil_kernel, bx_n, by_n),
        out_shape=[pltpu.HBM((levels, nx, ny), f32)]
        + [shaped((cap, width + 2 * LANES), bf16)] * n_gy,
        in_specs=vmem(11),
        out_specs=[any_hbm] + vmem(n_gy),
        scratch_shapes=[pltpu.VMEM((n_blocks, width), f32)]
        + [pltpu.VMEM((levels + SUB, LANES), f32)] * 2
        + [pltpu.VMEM((levels, nx, ny), f32), pltpu.SemaphoreType.DMA((levels // BATCH,))],
        compiler_params=params(),
        name="stencil",
    )(thermal, flags, tally, far_x1, far_x2, far_y1, far_y2, y1, y2, sel, tail)

    def swapped(x, d):
        return lax.ppermute(x, "gy", [(i, i ^ d) for i in range(n_gy)])

    came = [packed[0]]
    for d in range(1, n_gy):
        came.append(swapped(packed[d], d))

    arrived, weight, part = pl.pallas_call(
        functools.partial(growth_kernel, n_gy),
        out_shape=[
            shaped((slots, width + 2 * LANES), bf16),
            shaped((width // LANES, slots, LANES), f32),
            shaped((n_all, tracers, LANES), f32),
        ],
        in_specs=vmem(2 + n_gy),
        out_specs=vmem(3),
        compiler_params=params(),
        name="growth",
    )(
        pltpu.with_memory_space_constraint(above, pltpu.VMEM),
        pltpu.with_memory_space_constraint(held_amounts, pltpu.VMEM),
        *came,
    )

    parts = lax.all_to_all(part, ("gx", "gy"), 0, 0, tiled=True)
    returned = [passed[0]]
    for d in range(1, n_gy):
        returned.append(swapped(passed[d], d))

    mix = pl.pallas_call(
        mixing_kernel,
        out_shape=shaped((width // LANES, slots, LANES), f32),
        in_specs=vmem(1),
        out_specs=pl.BlockSpec(memory_space=pltpu.VMEM),
        compiler_params=params(),
        name="mixing",
    )(arrived)
    by_lane = pltpu.VMEM((width // LANES, group, LANES), f32)
    out, done = pl.pallas_call(
        functools.partial(final_kernel, cap),
        out_shape=[shaped((slots, tracers, width), f32), shaped((tracers, LANES), f32)],
        in_specs=vmem(4) + [any_hbm] * 2,
        out_specs=[any_hbm] + vmem(1),
        scratch_shapes=[
            buffers[0],
            pltpu.VMEM((tracers, tracers), f32),
            pltpu.VMEM((group * tracers, group * tracers), bf16),
            by_lane,
            pltpu.VMEM((group * tracers, width), f32),
            buffers[1],
            buffers[1],
            pltpu.SemaphoreType.DMA,
        ],
        compiler_params=params(),
        name="final",
    )(parts, arrived, weight, mix, in_hbm(reaction_rates), amounts)

    thermal_final = pl.pallas_call(
        functools.partial(warm_kernel, bx_n, by_n, n_gy),
        out_shape=shaped((levels, nx, ny), f32),
        in_specs=vmem(4) + [any_hbm] + vmem(1 + n_gy),
        out_specs=pl.BlockSpec(memory_space=pltpu.VMEM),
        scratch_shapes=[
            pltpu.VMEM((n_blocks, width), f32),
            pltpu.VMEM((levels, nx, ny), f32),
            pltpu.SemaphoreType.DMA,
        ],
        compiler_params=params(),
        name="warm",
    )(holder, light, flags, tally, in_hbm(stepped), done, *returned)
    return thermal_final, out.reshape(solute_amounts.shape)


def solution(mesh):
    return jax.shard_map(
        on_device,
        mesh=mesh,
        in_specs=(
            P(None, "gx", "gy"),
            P("gx", "gy"),
            P("gx", "gy"),
            P("gx", "gy", None),
            P("gx", "gy", None),
            P("gx", "gy", None, None),
            P("gx", "gy", None, None, None),
            P(),
        ),
        out_specs=(P(None, "gx", "gy"), P("gx", "gy", None, None, None)),
        check_vma=False,
    )
```

time: 78.1 us -> 64.1 us (0.82)
  waiting for transfers between devices: 21 us -> 3.14 us
  starting transfers between devices: 29.9 us -> 37.4 us
  Pallas kernels: 25.5 us -> 22.4 us
    all_to_all x1 -> x0, waiting for transfers between devices: 13.3 us -> none  [exchange(): y = lax.all_to_all(x.reshape(n_gy, cap, x.shape[1]), 'gy', 0, 0, tiled=True)]
    ppermute x11 -> x18, starting transfers between devices: 21.5 us -> 31.5 us  [the longest x14 27 us: swapped(): return lax.ppermute(x, 'gy', [(i, i ^ d) for i in range(n_gy)])]
    all_to_all x1 -> x0, starting transfers between devices: 5.75 us -> none  [exchange(): y = lax.all_to_all(x.reshape(n_gy, cap, x.shape[1]), 'gy', 0, 0, tiled=True)]
    ppermute x11 -> x18, waiting for transfers between devices: 7.71 us -> 3.14 us  [the longest x14 2.59 us: swapped(): return lax.ppermute(x, 'gy', [(i, i ^ d) for i in range(n_gy)])]
    all_to_all x1, starting transfers between devices: 2.7 us -> 5.91 us  [on_device(): parts = lax.all_to_all(part, ('gx', 'gy'), 0, 0, tiled=True)]
    pallas_call x4 -> x5, Pallas kernels: 18.1 us -> 15.6 us  [the longest x1 7.43 us: on_device(): pl.pallas_call(functools.partial(final_kernel, cap), out_shape=[shaped((s...]
    pallas_call x1, Pallas kernels: 3.25 us -> 2.31 us  [on_device(): pl.pallas_call(functools.partial(stencil_kernel, bx_n, by_n), out_shape=[...]
  transfers between devices with their start and end apart: 13 -> 19, of which waited for: 5 -> 2; matrix products, arithmetic and copies ran while one was open for 0% -> 0% of each run, Pallas kernels for 9% -> 21%
where the time goes in v2:
time: 64.1 us; the launch traced here: 63.8 us
  starting transfers between devices  37.4 us (58%)
  Pallas kernels  22.4 us (35%)
  waiting for transfers between devices  3.14 us (5%)
  between operations  0.83 us (1%)
    ppermute x14, starting transfers between devices, swapped(): return lax.ppermute(x, 'gy', [(i, i ^ d) for i in range(n_gy)])  27 us
    pallas_call x1, Pallas kernels, on_device(): pl.pallas_call(functools.partial(final_kernel, cap), out_shape=[shaped((s...  7.43 us
    all_to_all x1, starting transfers between devices, on_device(): parts = lax.all_to_all(part, ('gx', 'gy'), 0, 0, tiled=True)  5.91 us
    pallas_call x1, Pallas kernels, on_device(): pl.pallas_call(functools.partial(clear_kernel, n_gy), out_shape=[pltpu.VM...  4.55 us
    ppermute x4, starting transfers between devices, traded(): return lax.ppermute(x, axis, pairs + [(j, i) for i, j in pairs])  4.42 us
    pallas_call x1, Pallas kernels, on_device(): pl.pallas_call(functools.partial(warm_kernel, bx_n, by_n, n_gy), out_shap...  3.06 us
    ppermute x14, waiting for transfers between devices, swapped(): return lax.ppermute(x, 'gy', [(i, i ^ d) for i in range(n_gy)])  2.59 us
    pallas_call x1, Pallas kernels, on_device(): pl.pallas_call(functools.partial(stencil_kernel, bx_n, by_n), out_shape=[...  2.31 us
  transfers between devices with their start and end apart: 19, of which 2 were waited for; matrix products, arithmetic and copies ran while one was open for 0% of the time, Pallas kernels for 21%

profile of v2, /device:TPU:0, one launch (start us, length us, event | category | flops | bytes accessed | tf_op | source)
XLA Modules:
  0.0 63.8 jit_solution(11963973376164644947)
XLA Ops:
  0.6 1.4 %edges.1 = (f32[40,128]{1,0:T(8,128)S(1)}, f32[40,128]{1,0:T(8,128)S(1)}, f32[16,128]{1,0:T(8,128)S(1)}, f32[16,128]{1,0:T(8,128)S(1)}, f32[32,32,128]{2,1,0:T(8...) custom-call(f32[32,32,128]{2,1,0:T(8,128)} %refs_0_.1, ...), custom_call_target="tpu_custom_call" | custom-call | tf_op jit(solution)/shard_map/edges/pallas_call | solution.py:508
  2.1 0.6 collective-permute-start
  2.6 0.7 %collective-permute-start.1 = (f32[40,128]{1,0:T(8,128)S(1)}, f32[40,128]{1,0:T(8,128)S(1)}, u32[]{:S(2)}, u32[]{:S(2)}) collective-permute-start(f32[40,128]{1,0:T(8,128)S(1)} %get-tuple-element.44), channel_id=1, source_target_pairs={{8,16},{16,8},{9,17},{17,9},{10,18},{18,10},{11,19},{19,11},{12,20... | collective-permute-start | bytes 61448 | tf_op jit(solution)/shard_map/ppermute | solution.py:524
  3.3 2.6 %collective-permute-start.2 = (f32[16,128]{1,0:T(8,128)S(1)}, f32[16,128]{1,0:T(8,128)S(1)}, u32[]{:S(2)}, u32[]{:S(2)}) collective-permute-start(f32[16,128]{1,0:T(8,128)S(1)} %get-tuple-element.45.own_1), channel_id=1, source_target_pairs={{0,1},{2,3},{4,5},{6,7},{1,0},{3,2},{5,4},{7,6},{8,9},{10,11},{12,... | collective-permute-start | bytes 24584 | tf_op jit(solution)/shard_map/ppermute | solution.py:524
  5.9 0.6 %collective-permute-start.3 = (f32[16,128]{1,0:T(8,128)S(1)}, f32[16,128]{1,0:T(8,128)S(1)}, u32[]{:S(2)}, u32[]{:S(2)}) collective-permute-start(f32[16,128]{1,0:T(8,128)S(1)} %get-tuple-element.46.own_2), channel_id=1, source_target_pairs={{1,2},{3,4},{5,6},{2,1},{4,3},{6,5},{9,10},{11,12},{13,14},{10,9},... | collective-permute-start | bytes 24584 | tf_op jit(solution)/shard_map/ppermute | solution.py:524
  6.5 0.4 slots.1
  7.0 0.5 collective-permute-done.2.y1
  7.5 0.0 collective-permute-done.3.y2
  7.5 0.0 collective-permute-done.x1
  7.5 0.0 collective-permute-done.1.x2
  7.5 2.3 %stencil.1 = (f32[32,32,128]{2,1,0:T(8,128)}, bf16[16,2304]{1,0:T(8,128)(2,1)S(1)}, bf16[16,2304]{1,0:T(8,128)(2,1)S(1)}, bf16[16,2304]{1,0:T(8,128)(2,1)S(1)}, ...) custom-call(f32[32,32,128]{2,1,0:T(8,128)S(1)} %get-tuple-element.42, ...), custom_call_target="tpu_custom_call" | custom-call | tf_op jit(solution)/shard_map/stencil/pallas_call | solution.py:568
  9.8 5.0 %collective-permute-start.4 = (bf16[16,2304]{1,0:T(8,128)(2,1)S(1)}, bf16[16,2304]{1,0:T(8,128)(2,1)S(1)}, u32[]{:S(2)}, u32[]{:S(2)}) collective-permute-start(bf16[16,2304]{1,0:T(8,128)(2,1)S(1)} %get-tuple-element.54), channel_id=1, source_target_pairs={{0,1},{1,0},{2,3},{3,2},{4,5},{5,4},{6,7},{7,6},{8,9},{9,8},{10,11... | collective-permute-start | bytes 221192 | tf_op jit(solution)/shard_map/ppermute | solution.py:582
  14.8 2.0 %collective-permute-start.5 = (bf16[16,2304]{1,0:T(8,128)(2,1)S(1)}, bf16[16,2304]{1,0:T(8,128)(2,1)S(1)}, u32[]{:S(2)}, u32[]{:S(2)}) collective-permute-start(bf16[16,2304]{1,0:T(8,128)(2,1)S(1)} %get-tuple-element.55), channel_id=1, source_target_pairs={{0,2},{1,3},{2,0},{3,1},{4,6},{5,7},{6,4},{7,5},{8,10},{9,11},{10,... | collective-permute-start | bytes 221192 | tf_op jit(solution)/shard_map/ppermute | solution.py:582
  16.8 0.9 %collective-permute-start.6 = (bf16[16,2304]{1,0:T(8,128)(2,1)S(1)}, bf16[16,2304]{1,0:T(8,128)(2,1)S(1)}, u32[]{:S(2)}, u32[]{:S(2)}) collective-permute-start(bf16[16,2304]{1,0:T(8,128)(2,1)S(1)} %get-tuple-element.56), channel_id=1, source_target_pairs={{0,3},{1,2},{2,1},{3,0},{4,7},{5,6},{6,5},{7,4},{8,11},{9,10},{10,... | collective-permute-start | bytes 221192 | tf_op jit(solution)/shard_map/ppermute | solution.py:582
  17.7 3.0 %collective-permute-start.7 = (bf16[16,2304]{1,0:T(8,128)(2,1)S(1)}, bf16[16,2304]{1,0:T(8,128)(2,1)S(1)}, u32[]{:S(2)}, u32[]{:S(2)}) collective-permute-start(bf16[16,2304]{1,0:T(8,128)(2,1)S(1)} %get-tuple-element.57), channel_id=1, source_target_pairs={{0,4},{1,5},{2,6},{3,7},{4,0},{5,1},{6,2},{7,3},{8,12},{9,13},{10,... | collective-permute-start | bytes 221192 | tf_op jit(solution)/shard_map/ppermute | solution.py:582
  20.8 0.0 collective-permute-start.8
  20.8 0.0 collective-permute-done.4.rest_1_
  20.8 3.5 %collective-permute-start.9 = (bf16[16,2304]{1,0:T(8,128)(2,1)S(1)}, bf16[16,2304]{1,0:T(8,128)(2,1)S(1)}, u32[]{:S(2)}, u32[]{:S(2)}) collective-permute-start(bf16[16,2304]{1,0:T(8,128)(2,1)S(1)} %get-tuple-element.59), channel_id=1, source_target_pairs={{0,6},{1,7},{2,4},{3,5},{4,2},{5,3},{6,0},{7,1},{8,14},{9,15},{10,... | collective-permute-start | bytes 221192 | tf_op jit(solution)/shard_map/ppermute | solution.py:582
  24.2 0.0 collective-permute-done.5.rest_2_
  24.2 1.5 %collective-permute-start.10 = (bf16[16,2304]{1,0:T(8,128)(2,1)S(1)}, bf16[16,2304]{1,0:T(8,128)(2,1)S(1)}, u32[]{:S(2)}, u32[]{:S(2)}) collective-permute-start(bf16[16,2304]{1,0:T(8,128)(2,1)S(1)} %get-tuple-element.60), channel_id=1, source_target_pairs={{0,7},{1,6},{2,5},{3,4},{4,3},{5,2},{6,1},{7,0},{8,15},{9,14},{10,... | collective-permute-start | bytes 221192 | tf_op jit(solution)/shard_map/ppermute | solution.py:582
  25.7 4.5 %clear.1 = (f32[128,2048]{1,0:T(8,128)S(1)}, f32[8,16,8,2048]{3,2,1,0:T(8,128)S(1)}, bf16[16,2048]{1,0:T(8,128)(2,1)}, bf16[16,2048]{1,0:T(8,128)(2,1)}, bf16[16...) custom-call(f32[128,8,2048]{2,1,0:T(8,128)} %bitcast.5), custom_call_target="tpu_custom_call" | custom-call | tf_op jit(solution)/shard_map/clear/pallas_call | solution.py:550
  30.2 0.0 copy-start.4
  30.2 0.0 copy-start.3
  30.3 0.0 collective-permute-done.6.rest_3_
  30.3 0.0 collective-permute-done.7.rest_4_
  30.3 2.6 %collective-permute-done.8.rest_5_ = bf16[16,2304]{1,0:T(8,128)(2,1)S(1)} collective-permute-done((bf16[16,2304]{1,0:T(8,128)(2,1)S(1)}, bf16[16,2304]{1,0:T(8,128)(2,1)S(1)}, u32[]{:S(2)}, u32[]{:S(2)}) %collective-permute-start.8) | collective-permute-done | bytes 73760 | tf_op jit(solution)/shard_map/ppermute | solution.py:582
  32.9 0.0 collective-permute-done.9.rest_6_
  32.9 0.0 collective-permute-done.10.rest_7_
  32.9 2.2 %growth.1 = (bf16[128,2304]{1,0:T(8,128)(2,1)S(1)}, f32[16,128,128]{2,1,0:T(8,128)S(1)}, f32[32,8,128]{2,1,0:T(8,128)}) custom-call(f32[128,2048]{1,0:T(8,128)S(1)} %get-tuple-element.51.above, f32[8,16,8,2048]{3,2,1,0:T(8,128)S(1)} %get-tuple-element.52.c, bf16[16,2304]{1,0:T(8,128)(2,1)S(1)} %get-tuple-element.53.rest_0_, ...), custom_call_target="tpu_custom_call" | custom-call | tf_op jit(solution)/shard_map/growth/pallas_call | solution.py:588
  35.1 5.9 %all-to-all-start = ((f32[32,8,128]{2,1,0:T(8,128)}), f32[32,8,128]{2,1,0:T(8,128)S(1)}, u32[]{:S(2)}, u32[]{:S(2)}) async-start(f32[32,8,128]{2,1,0:T(8,128)} %get-tuple-element.61), calls=%async_computation | async-start | bytes 262144 | tf_op jit(solution)/shard_map/all_to_all | solution.py:605
  41.0 1.8 %collective-permute-start.11 = (bf16[16,2048]{1,0:T(8,128)(2,1)S(1)}, bf16[16,2048]{1,0:T(8,128)(2,1)S(1)}, u32[]{:S(2)}, u32[]{:S(2)}) collective-permute-start(bf16[16,2048]{1,0:T(8,128)(2,1)S(1)} %copy-done.4), channel_id=1, source_target_pairs={{0,1},{1,0},{2,3},{3,2},{4,5},{5,4},{6,7},{7,6},{8,9},{9,8},{10,11... | collective-permute-start | bytes 196616 | tf_op jit(solution)/shard_map/ppermute | solution.py:582
  42.8 1.5 %collective-permute-start.12 = (bf16[16,2048]{1,0:T(8,128)(2,1)S(1)}, bf16[16,2048]{1,0:T(8,128)(2,1)S(1)}, u32[]{:S(2)}, u32[]{:S(2)}) collective-permute-start(bf16[16,2048]{1,0:T(8,128)(2,1)S(1)} %copy-done.3), channel_id=1, source_target_pairs={{0,2},{1,3},{2,0},{3,1},{4,6},{5,7},{6,4},{7,5},{8,10},{9,11},{10,... | collective-permute-start | bytes 196616 | tf_op jit(solution)/shard_map/ppermute | solution.py:582
  44.3 0.3 collective-permute-start.13
  44.6 2.7 %collective-permute-start.14 = (bf16[16,2048]{1,0:T(8,128)(2,1)}, bf16[16,2048]{1,0:T(8,128)(2,1)S(1)}, u32[]{:S(2)}, u32[]{:S(2)}) collective-permute-start(bf16[16,2048]{1,0:T(8,128)(2,1)} %get-tuple-element.69), channel_id=1, source_target_pairs={{0,4},{1,5},{2,6},{3,7},{4,0},{5,1},{6,2},{7,3},{8,12},{9,13},{10,... | collective-permute-start | bytes 196616 | tf_op jit(solution)/shard_map/ppermute | solution.py:582
  47.2 1.5 %collective-permute-start.15 = (bf16[16,2048]{1,0:T(8,128)(2,1)}, bf16[16,2048]{1,0:T(8,128)(2,1)S(1)}, u32[]{:S(2)}, u32[]{:S(2)}) collective-permute-start(bf16[16,2048]{1,0:T(8,128)(2,1)} %get-tuple-element.70), channel_id=1, source_target_pairs={{0,5},{1,4},{2,7},{3,6},{4,1},{5,0},{6,3},{7,2},{8,13},{9,12},{10,... | collective-permute-start | bytes 196616 | tf_op jit(solution)/shard_map/ppermute | solution.py:582
  48.7 0.0 collective-permute-done.11.rest_1_
  48.7 3.3 %collective-permute-start.16 = (bf16[16,2048]{1,0:T(8,128)(2,1)S(1)}, bf16[16,2048]{1,0:T(8,128)(2,1)S(1)}, u32[]{:S(2)}, u32[]{:S(2)}) collective-permute-start(bf16[16,2048]{1,0:T(8,128)(2,1)S(1)} %copy-done.2), channel_id=1, source_target_pairs={{0,6},{1,7},{2,4},{3,5},{4,2},{5,3},{6,0},{7,1},{8,14},{9,15},{10,... | collective-permute-start | bytes 196616 | tf_op jit(solution)/shard_map/ppermute | solution.py:582
  52.0 0.0 collective-permute-done.12.rest_2_
  52.0 0.2 collective-permute-start.17
  52.2 1.0 %mixing.1.mix = f32[16,128,128]{2,1,0:T(8,128)S(1)} custom-call(bf16[128,2304]{1,0:T(8,128)(2,1)S(1)} %get-tuple-element.62.arrived), custom_call_target="tpu_custom_call" | custom-call | tf_op jit(solution)/shard_map/mixing/pallas_call | solution.py:610
  53.2 0.0 all-to-all-done.parts
  53.2 7.4 %final.1 = (f32[128,8,2048]{2,1,0:T(8,128)}, f32[8,128]{1,0:T(8,128)S(1)}) custom-call(f32[32,8,128]{2,1,0:T(8,128)S(1)} %all-to-all-done.parts, bf16[128,2304]{1,0:T(8,128)(2,1)S(1)} %get-tuple-element.62.arrived, f32[16,128,128]{2,1,0:T(8,128)S(1)} %get-tuple-element.63.weight, f32[16,128,128]{2,1,0:T(8,128)S(1)} %mixing.1.mix, f32[8,8]{1,0:T(8,128)} %rates_hbm.1, ...), custom_call_target="tpu_custom_call" | custom-call | tf_op jit(solution)/shard_map/final/pallas_call | solution.py:619
  60.7 0.0 collective-permute-done.13.rest_3_
  60.7 0.0 collective-permute-done.14.rest_4_
  60.7 0.0 collective-permute-done.15.rest_5_
  60.7 0.0 collective-permute-done.16.rest_6_
  60.7 0.0 collective-permute-done.17.rest_7_
  60.7 3.1 %warm.1 = f32[32,32,128]{2,1,0:T(8,128)} custom-call(s32[1,64]{1,0:T(1,128)S(1)} %get-tuple-element.38.holder, bf16[32,128]{1,0:T(8,128)(2,1)S(1)} %get-tuple-element.39.light, s32[1,64]{1,0:T(1,128)S(1)} %get-tuple-element.40.flags, s32[1,64]{1,0:T(1,128)S(1)} %get-tuple-element.41.tally, f32[32,32,128]{2,1,0:T(8,128)} %get-tuple-element.50.stepped_hbm, ...), custom_call_target="tpu_custom_call" | custom-call | tf_op jit(solution)/shard_map/warm/pallas_call | solution.py:638
  (8 shorter events, 0.0 us)
Async XLA Ops:
  2.1 5.4 %collective-permute-start = (f32[40,128]{1,0:T(8,128)S(1)}, f32[40,128]{1,0:T(8,128)S(1)}, u32[]{:S(2)}, u32[]{:S(2)}) collective-permute-start(f32[40,128]{1,0:T(8,128)S(1)} %get-tuple-element.43), channel_id=1, source_target_pairs={{0,8},{16,24},{8,0},{24,16},{1,9},{17,25},{9,1},{25,17},{2,10},{18... | collective-permute-start | bytes 61448 | tf_op jit(solution)/shard_map/ppermute | solution.py:524
  2.6 4.9 %collective-permute-start.1 = (f32[40,128]{1,0:T(8,128)S(1)}, f32[40,128]{1,0:T(8,128)S(1)}, u32[]{:S(2)}, u32[]{:S(2)}) collective-permute-start(f32[40,128]{1,0:T(8,128)S(1)} %get-tuple-element.44), channel_id=1, source_target_pairs={{8,16},{16,8},{9,17},{17,9},{10,18},{18,10},{11,19},{19,11},{12,20... | collective-permute-start | bytes 61448 | tf_op jit(solution)/shard_map/ppermute | solution.py:524
  3.3 4.2 %collective-permute-start.2 = (f32[16,128]{1,0:T(8,128)S(1)}, f32[16,128]{1,0:T(8,128)S(1)}, u32[]{:S(2)}, u32[]{:S(2)}) collective-permute-start(f32[16,128]{1,0:T(8,128)S(1)} %get-tuple-element.45.own_1), channel_id=1, source_target_pairs={{0,1},{2,3},{4,5},{6,7},{1,0},{3,2},{5,4},{7,6},{8,9},{10,11},{12,... | collective-permute-start | bytes 24584 | tf_op jit(solution)/shard_map/ppermute | solution.py:524
  5.9 1.6 %collective-permute-start.3 = (f32[16,128]{1,0:T(8,128)S(1)}, f32[16,128]{1,0:T(8,128)S(1)}, u32[]{:S(2)}, u32[]{:S(2)}) collective-permute-start(f32[16,128]{1,0:T(8,128)S(1)} %get-tuple-element.46.own_2), channel_id=1, source_target_pairs={{1,2},{3,4},{5,6},{2,1},{4,3},{6,5},{9,10},{11,12},{13,14},{10,9},... | collective-permute-start | bytes 24584 | tf_op jit(solution)/shard_map/ppermute | solution.py:524
  9.8 10.9 %collective-permute-start.4 = (bf16[16,2304]{1,0:T(8,128)(2,1)S(1)}, bf16[16,2304]{1,0:T(8,128)(2,1)S(1)}, u32[]{:S(2)}, u32[]{:S(2)}) collective-permute-start(bf16[16,2304]{1,0:T(8,128)(2,1)S(1)} %get-tuple-element.54), channel_id=1, source_target_pairs={{0,1},{1,0},{2,3},{3,2},{4,5},{5,4},{6,7},{7,6},{8,9},{9,8},{10,11... | collective-permute-start | bytes 221192 | tf_op jit(solution)/shard_map/ppermute | solution.py:582
  14.8 9.4 %collective-permute-start.5 = (bf16[16,2304]{1,0:T(8,128)(2,1)S(1)}, bf16[16,2304]{1,0:T(8,128)(2,1)S(1)}, u32[]{:S(2)}, u32[]{:S(2)}) collective-permute-start(bf16[16,2304]{1,0:T(8,128)(2,1)S(1)} %get-tuple-element.55), channel_id=1, source_target_pairs={{0,2},{1,3},{2,0},{3,1},{4,6},{5,7},{6,4},{7,5},{8,10},{9,11},{10,... | collective-permute-start | bytes 221192 | tf_op jit(solution)/shard_map/ppermute | solution.py:582
  16.8 13.5 %collective-permute-start.6 = (bf16[16,2304]{1,0:T(8,128)(2,1)S(1)}, bf16[16,2304]{1,0:T(8,128)(2,1)S(1)}, u32[]{:S(2)}, u32[]{:S(2)}) collective-permute-start(bf16[16,2304]{1,0:T(8,128)(2,1)S(1)} %get-tuple-element.56), channel_id=1, source_target_pairs={{0,3},{1,2},{2,1},{3,0},{4,7},{5,6},{6,5},{7,4},{8,11},{9,10},{10,... | collective-permute-start | bytes 221192 | tf_op jit(solution)/shard_map/ppermute | solution.py:582
  17.7 12.6 %collective-permute-start.7 = (bf16[16,2304]{1,0:T(8,128)(2,1)S(1)}, bf16[16,2304]{1,0:T(8,128)(2,1)S(1)}, u32[]{:S(2)}, u32[]{:S(2)}) collective-permute-start(bf16[16,2304]{1,0:T(8,128)(2,1)S(1)} %get-tuple-element.57), channel_id=1, source_target_pairs={{0,4},{1,5},{2,6},{3,7},{4,0},{5,1},{6,2},{7,3},{8,12},{9,13},{10,... | collective-permute-start | bytes 221192 | tf_op jit(solution)/shard_map/ppermute | solution.py:582
  20.8 12.1 %collective-permute-start.8 = (bf16[16,2304]{1,0:T(8,128)(2,1)S(1)}, bf16[16,2304]{1,0:T(8,128)(2,1)S(1)}, u32[]{:S(2)}, u32[]{:S(2)}) collective-permute-start(bf16[16,2304]{1,0:T(8,128)(2,1)S(1)} %get-tuple-element.58), channel_id=1, source_target_pairs={{0,5},{1,4},{2,7},{3,6},{4,1},{5,0},{6,3},{7,2},{8,13},{9,12},{10,... | collective-permute-start | bytes 221192 | tf_op jit(solution)/shard_map/ppermute | solution.py:582
  20.8 12.1 %collective-permute-start.9 = (bf16[16,2304]{1,0:T(8,128)(2,1)S(1)}, bf16[16,2304]{1,0:T(8,128)(2,1)S(1)}, u32[]{:S(2)}, u32[]{:S(2)}) collective-permute-start(bf16[16,2304]{1,0:T(8,128)(2,1)S(1)} %get-tuple-element.59), channel_id=1, source_target_pairs={{0,6},{1,7},{2,4},{3,5},{4,2},{5,3},{6,0},{7,1},{8,14},{9,15},{10,... | collective-permute-start | bytes 221192 | tf_op jit(solution)/shard_map/ppermute | solution.py:582
  24.2 8.6 %collective-permute-start.10 = (bf16[16,2304]{1,0:T(8,128)(2,1)S(1)}, bf16[16,2304]{1,0:T(8,128)(2,1)S(1)}, u32[]{:S(2)}, u32[]{:S(2)}) collective-permute-start(bf16[16,2304]{1,0:T(8,128)(2,1)S(1)} %get-tuple-element.60), channel_id=1, source_target_pairs={{0,7},{1,6},{2,5},{3,4},{4,3},{5,2},{6,1},{7,0},{8,15},{9,14},{10,... | collective-permute-start | bytes 221192 | tf_op jit(solution)/shard_map/ppermute | solution.py:582
  30.2 10.8 %copy-start.4 = (bf16[16,2048]{1,0:T(8,128)(2,1)S(1)}, bf16[16,2048]{1,0:T(8,128)(2,1)}, u32[]{:S(2)}) copy-start(bf16[16,2048]{1,0:T(8,128)(2,1)} %get-tuple-element.66) | copy-start | bytes 196612
  30.2 12.6 %copy-start.3 = (bf16[16,2048]{1,0:T(8,128)(2,1)S(1)}, bf16[16,2048]{1,0:T(8,128)(2,1)}, u32[]{:S(2)}) copy-start(bf16[16,2048]{1,0:T(8,128)(2,1)} %get-tuple-element.67) | copy-start | bytes 196612
  30.3 18.4 %copy-start.2 = (bf16[16,2048]{1,0:T(8,128)(2,1)S(1)}, bf16[16,2048]{1,0:T(8,128)(2,1)}, u32[]{:S(2)}) copy-start(bf16[16,2048]{1,0:T(8,128)(2,1)} %get-tuple-element.71) | copy-start | bytes 196612
  30.3 21.8 %copy-start.1 = (bf16[16,2048]{1,0:T(8,128)(2,1)S(1)}, bf16[16,2048]{1,0:T(8,128)(2,1)}, u32[]{:S(2)}) copy-start(bf16[16,2048]{1,0:T(8,128)(2,1)} %get-tuple-element.72) | copy-start | bytes 196612
  35.1 25.6 %copy-start = (bf16[16,2048]{1,0:T(8,128)(2,1)S(1)}, bf16[16,2048]{1,0:T(8,128)(2,1)}, u32[]{:S(2)}) copy-start(bf16[16,2048]{1,0:T(8,128)(2,1)} %get-tuple-element.65.rest_0_) | copy-start | bytes 196612
  35.1 18.1 %all-to-all-start = ((f32[32,8,128]{2,1,0:T(8,128)}), f32[32,8,128]{2,1,0:T(8,128)S(1)}, u32[]{:S(2)}, u32[]{:S(2)}) async-start(f32[32,8,128]{2,1,0:T(8,128)} %get-tuple-element.61), calls=%async_computation | async-start | bytes 262144 | tf_op jit(solution)/shard_map/all_to_all | solution.py:605
  41.0 7.7 %collective-permute-start.11 = (bf16[16,2048]{1,0:T(8,128)(2,1)S(1)}, bf16[16,2048]{1,0:T(8,128)(2,1)S(1)}, u32[]{:S(2)}, u32[]{:S(2)}) collective-permute-start(bf16[16,2048]{1,0:T(8,128)(2,1)S(1)} %copy-done.4), channel_id=1, source_target_pairs={{0,1},{1,0},{2,3},{3,2},{4,5},{5,4},{6,7},{7,6},{8,9},{9,8},{10,11... | collective-permute-start | bytes 196616 | tf_op jit(solution)/shard_map/ppermute | solution.py:582
  42.8 9.2 %collective-permute-start.12 = (bf16[16,2048]{1,0:T(8,128)(2,1)S(1)}, bf16[16,2048]{1,0:T(8,128)(2,1)S(1)}, u32[]{:S(2)}, u32[]{:S(2)}) collective-permute-start(bf16[16,2048]{1,0:T(8,128)(2,1)S(1)} %copy-done.3), channel_id=1, source_target_pairs={{0,2},{1,3},{2,0},{3,1},{4,6},{5,7},{6,4},{7,5},{8,10},{9,11},{10,... | collective-permute-start | bytes 196616 | tf_op jit(solution)/shard_map/ppermute | solution.py:582
  44.3 16.3 %collective-permute-start.13 = (bf16[16,2048]{1,0:T(8,128)(2,1)}, bf16[16,2048]{1,0:T(8,128)(2,1)S(1)}, u32[]{:S(2)}, u32[]{:S(2)}) collective-permute-start(bf16[16,2048]{1,0:T(8,128)(2,1)} %get-tuple-element.68), channel_id=1, source_target_pairs={{0,3},{1,2},{2,1},{3,0},{4,7},{5,6},{6,5},{7,4},{8,11},{9,10},{10,... | collective-permute-start | bytes 196616 | tf_op jit(solution)/shard_map/ppermute | solution.py:582
  44.6 16.1 %collective-permute-start.14 = (bf16[16,2048]{1,0:T(8,128)(2,1)}, bf16[16,2048]{1,0:T(8,128)(2,1)S(1)}, u32[]{:S(2)}, u32[]{:S(2)}) collective-permute-start(bf16[16,2048]{1,0:T(8,128)(2,1)} %get-tuple-element.69), channel_id=1, source_target_pairs={{0,4},{1,5},{2,6},{3,7},{4,0},{5,1},{6,2},{7,3},{8,12},{9,13},{10,... | collective-permute-start | bytes 196616 | tf_op jit(solution)/shard_map/ppermute | solution.py:582
  47.2 13.4 %collective-permute-start.15 = (bf16[16,2048]{1,0:T(8,128)(2,1)}, bf16[16,2048]{1,0:T(8,128)(2,1)S(1)}, u32[]{:S(2)}, u32[]{:S(2)}) collective-permute-start(bf16[16,2048]{1,0:T(8,128)(2,1)} %get-tuple-element.70), channel_id=1, source_target_pairs={{0,5},{1,4},{2,7},{3,6},{4,1},{5,0},{6,3},{7,2},{8,13},{9,12},{10,... | collective-permute-start | bytes 196616 | tf_op jit(solution)/shard_map/ppermute | solution.py:582
  48.7 12.0 %collective-permute-start.16 = (bf16[16,2048]{1,0:T(8,128)(2,1)S(1)}, bf16[16,2048]{1,0:T(8,128)(2,1)S(1)}, u32[]{:S(2)}, u32[]{:S(2)}) collective-permute-start(bf16[16,2048]{1,0:T(8,128)(2,1)S(1)} %copy-done.2), channel_id=1, source_target_pairs={{0,6},{1,7},{2,4},{3,5},{4,2},{5,3},{6,0},{7,1},{8,14},{9,15},{10,... | collective-permute-start | bytes 196616 | tf_op jit(solution)/shard_map/ppermute | solution.py:582
  52.0 8.7 %collective-permute-start.17 = (bf16[16,2048]{1,0:T(8,128)(2,1)S(1)}, bf16[16,2048]{1,0:T(8,128)(2,1)S(1)}, u32[]{:S(2)}, u32[]{:S(2)}) collective-permute-start(bf16[16,2048]{1,0:T(8,128)(2,1)S(1)} %copy-done.1), channel_id=1, source_target_pairs={{0,7},{1,6},{2,5},{3,4},{4,3},{5,2},{6,1},{7,0},{8,15},{9,14},{10,... | collective-permute-start | bytes 196616 | tf_op jit(solution)/shard_map/ppermute | solution.py:582

commit v3 on v2

--- a/solution.py
+++ b/solution.py
@@ -12,6 +12,8 @@
 ATTEN_CHL = 0.05
 WARMING_SCALE = 0.5
 GROWTH_TEMP = 0.063
+DRY = 2.0**100
+WET = 2.0**50
 LANES = 128
 HALF = 64
 SUB = 8
@@ -127,25 +129,18 @@
     return own, rank_row, own_col, rank_col
 
 
-def slots_kernel(bx_n, by_n, cap, amb, light, flags, tally, holder, sel, tail):
+def slots_kernel(bx_n, by_n, cap, amb, light, holder, sel, tail):
     n = bx_n * by_n
     slots = sel.shape[0]
     _, rank_row, _, _ = ranks(holder)
     turn = jnp.bitwise_xor(holder[...], lax.axis_index("gy")).astype(f32)
     chosen = (iota((slots, n), 0).astype(f32) == turn * cap + rank_row).astype(bf16)
     sel[...] = chosen
-    row_i = iota((n, n), 0)
-    col_i = iota((n, n), 1)
-    depth = (flags[...] * tally[...]).astype(f32)
-    depth_col = jnp.sum(
-        jnp.where(row_i == col_i, jnp.broadcast_to(depth, (n, n)), 0.0), axis=1, keepdims=True
-    )
     a = amb[...].astype(f32).reshape(bx_n, SUB, LANES)
     b = light[...].astype(f32).reshape(bx_n, SUB, LANES)
     halves = jnp.stack(join_levels(a, b), axis=1).reshape(2 * bx_n, SUB, LANES)
-    rows = swap_granules(halves).reshape(n, LANES)
-    fields = jnp.concatenate([rows, jnp.broadcast_to(depth_col, (n, LANES))], axis=1).astype(bf16)
-    tail[...] = jnp.dot(chosen, fields, preferred_element_type=f32).astype(bf16)
+    rows = swap_granules(halves).reshape(n, LANES).astype(bf16)
+    tail[...] = jnp.dot(chosen, rows, preferred_element_type=f32).astype(bf16)
 
 
 def stencil_kernel(
@@ -217,7 +212,16 @@
             for bx in range(bx_n):
                 g = (bx * 2 + q % 2) * SUB
                 blocks[g : g + SUB, kp * LANES : (kp + 1) * LANES] = out[q * bx_n + bx]
-    chosen = jnp.dot(sel[...], blocks[...].astype(bf16), preferred_element_type=f32).astype(bf16)
+    n = depth.shape[1]
+    diagonal = iota((n, n), 0) == iota((n, n), 1)
+    depth_col = jnp.sum(
+        jnp.where(diagonal, jnp.broadcast_to(depth, (n, n)), 0.0), axis=1, keepdims=True
+    )
+    wet = (iota((n, width), 1) // HALF).astype(f32) < depth_col
+    marked = jnp.where(wet, blocks[...], DRY).astype(bf16)
+    taken = jnp.sum(sel[...].astype(f32), axis=1, keepdims=True) > 0
+    chosen = jnp.dot(sel[...], marked, preferred_element_type=f32)
+    chosen = jnp.where(taken, chosen, DRY).astype(bf16)
     cap = packed[0].shape[0]
     for i, chunk in enumerate(packed):
         chunk[:, :width] = chosen[i * cap : (i + 1) * cap]
@@ -262,30 +266,34 @@
 
 
 def spread_tail(arrived, rows, width):
-    tail = arrived[rows, width : width + LANES].astype(f32)
-    count = arrived[rows, width + LANES :].astype(f32)
+    tail = arrived[rows, width:].astype(f32)
     low = iota(tail.shape, 1) < HALF
     turned = pltpu.roll(tail, HALF, 1)
-    return jnp.where(low, tail, turned), jnp.where(low, turned, tail), count
+    return jnp.where(low, tail, turned), jnp.where(low, turned, tail)
 
 
 def growth_kernel(n_gy, above, c, *rest):
-    came, (arrived, weight, part) = rest[:n_gy], rest[n_gy:]
+    came, (arrived, counts_out, weight, part) = rest[:n_gy], rest[n_gy:]
     chunks, group, tracers, width = c.shape
     for i, chunk in enumerate(came):
         arrived[i * group : (i + 1) * group, :] = chunk[...]
     spans = [slice(v * LANES, (v + 1) * LANES) for v in range(width // LANES)]
-    half = (iota((group, LANES), 1) // HALF).astype(f32)
 
     def weigh(i):
         rows = pl.ds(pl.multiple_of(i * group, group), group)
-        _, light, count = spread_tail(arrived, rows, width)
+        _, light = spread_tail(arrived, rows, width)
+        sent = [arrived[rows, at].astype(f32) for at in spans]
+        wet = [x < WET for x in sent]
+        ones = [jnp.where(x, 1.0 / HALF, 0.0) for x in wet]
+        count = jnp.sum(functools.reduce(jnp.add, ones), axis=1, keepdims=True)
+        count = jnp.broadcast_to(count, (group, LANES))
+        counts_out[rows, :] = count
         tops = [light * above[rows, at] for at in spans]
-        temp = [jnp.exp(GROWTH_TEMP * arrived[rows, at].astype(f32)) for at in spans]
+        temp = [jnp.exp(GROWTH_TEMP * x) for x in sent]
         rest = [1.0 / (x + 1.0) for x in tops]
         for v in range(len(spans)):
             g = STEP_DT * (temp[v] * (tops[v] * rest[v]))
-            weight[v, rows, :] = jnp.where(half + float(2 * v) < count, g, 0.0)
+            weight[v, rows, :] = jnp.where(wet[v], g, 0.0)
         return count
 
     def gather(i, sums):
@@ -310,7 +318,7 @@
     part[...] = jnp.broadcast_to(line[None], part.shape)
 
 
-def mixing_kernel(arrived, mix):
+def mixing_kernel(arrived, counts, mix):
     steps, slots, _ = mix.shape
     width = steps * LANES
     group = 16
@@ -320,7 +328,8 @@
 
     def one(i, carry):
         rows = pl.ds(pl.multiple_of(i * group, group), group)
-        amb, _, count = spread_tail(arrived, rows, width)
+        amb, _ = spread_tail(arrived, rows, width)
+        count = counts[rows, :]
         here = [arrived[rows, at].astype(f32) for at in spans]
         below = [
             pltpu.roll(jnp.where(low, y, x), HALF, 1) for x, y in zip(here, here[1:] + here[-1:])
@@ -335,7 +344,7 @@
 
 
 def final_kernel(
-    cap, parts, arrived, weight, mix, rates_hbm, c, out, done, buf, rates, reactions, mix_up, mixed,
+    cap, parts, counts, weight, mix, rates_hbm, c, out, done, buf, rates, reactions, mix_up, mixed,
     sems, out_sems, rates_sem,
 ):
     chunks, group, tracers, width = buf.shape
@@ -390,7 +399,7 @@
 
         source, kept_at, goes = load(i)
         pltpu.make_async_copy(source, kept_at, sems.at[i]).wait()
-        count = arrived[rows, width + LANES :].astype(f32)
+        count = counts[rows, :]
         kept = [mix[v, rows, :] for v in range(steps)]
         zero = jnp.zeros_like(kept[0])
         for v, (x, y) in enumerate(zip(kept, [zero] + kept[:-1])):
@@ -430,10 +439,8 @@
         pltpu.make_async_copy(kept_at, goes, out_sems.at[i]).wait()
 
 
-def warm_kernel(bx_n, by_n, n_gy, holder, light, flags, tally, stepped_hbm, _, *rest):
-    returned, (out, blocks, stepped, sem) = rest[:n_gy], rest[n_gy:]
-    fetch = pltpu.make_async_copy(stepped_hbm, stepped, sem)
-    fetch.start()
+def warm_kernel(bx_n, by_n, n_gy, holder, light, flags, tally, stepped, _, *rest):
+    returned, (out_hbm, blocks, out, sems) = rest[:n_gy], rest[n_gy:]
     levels, nx, ny = stepped.shape
     cap = returned[0].shape[0]
     n = bx_n * by_n
@@ -449,7 +456,7 @@
         [jnp.broadcast_to(d[bx : bx + 1], (SUB, LANES)) for bx in range(bx_n)], axis=0
     )
     scale = WARMING_SCALE * light[...].astype(f32)
-    fetch.wait()
+    sends = []
     for k0 in range(0, levels, WARM_BATCH):
         halves = []
         for q in range(WARM_BATCH):
@@ -464,6 +471,11 @@
             for e, took in enumerate(join_levels(lo, hi)):
                 k = k0 + 2 * p + e
                 out[k] = stepped[k] + jnp.where(d_at > float(k), scale * took.reshape(nx, ny), 0.0)
+        rows = pl.ds(k0, WARM_BATCH)
+        sends.append(pltpu.make_async_copy(out.at[rows], out_hbm.at[rows], sems.at[len(sends)]))
+        sends[-1].start()
+    for send in sends:
+        send.wait()
 
 
 def vmem(n):
@@ -532,13 +544,13 @@
         functools.partial(slots_kernel, bx_n, by_n, cap),
         out_shape=[
             shaped((slots, n_blocks), bf16),
-            shaped((slots, 2 * LANES), bf16),
+            shaped((slots, LANES), bf16),
         ],
-        in_specs=vmem(5),
+        in_specs=vmem(3),
         out_specs=vmem(2),
         compiler_params=params(),
         name="slots",
-    )(ambient, light, flags, tally, holder)
+    )(ambient, light, holder)
 
     group = min(16, cap)
     steps = slots // group
@@ -568,7 +580,7 @@
     stepped, *packed = pl.pallas_call(
         functools.partial(stencil_kernel, bx_n, by_n),
         out_shape=[pltpu.HBM((levels, nx, ny), f32)]
-        + [shaped((cap, width + 2 * LANES), bf16)] * n_gy,
+        + [shaped((cap, width + LANES), bf16)] * n_gy,
         in_specs=vmem(11),
         out_specs=[any_hbm] + vmem(n_gy),
         scratch_shapes=[pltpu.VMEM((n_blocks, width), f32)]
@@ -585,15 +597,16 @@
     for d in range(1, n_gy):
         came.append(swapped(packed[d], d))
 
-    arrived, weight, part = pl.pallas_call(
+    arrived, counts, weight, part = pl.pallas_call(
         functools.partial(growth_kernel, n_gy),
         out_shape=[
-            shaped((slots, width + 2 * LANES), bf16),
+            shaped((slots, width + LANES), bf16),
+            shaped((slots, LANES), f32),
             shaped((width // LANES, slots, LANES), f32),
             shaped((n_all, tracers, LANES), f32),
         ],
         in_specs=vmem(2 + n_gy),
-        out_specs=vmem(3),
+        out_specs=vmem(4),
         compiler_params=params(),
         name="growth",
     )(
@@ -610,11 +623,11 @@
     mix = pl.pallas_call(
         mixing_kernel,
         out_shape=shaped((width // LANES, slots, LANES), f32),
-        in_specs=vmem(1),
+        in_specs=vmem(2),
         out_specs=pl.BlockSpec(memory_space=pltpu.VMEM),
         compiler_params=params(),
         name="mixing",
-    )(arrived)
+    )(arrived, counts)
     by_lane = pltpu.VMEM((width // LANES, group, LANES), f32)
     out, done = pl.pallas_call(
         functools.partial(final_kernel, cap),
@@ -633,21 +646,21 @@
         ],
         compiler_params=params(),
         name="final",
-    )(parts, arrived, weight, mix, in_hbm(reaction_rates), amounts)
+    )(parts, counts, weight, mix, in_hbm(reaction_rates), amounts)
 
     thermal_final = pl.pallas_call(
         functools.partial(warm_kernel, bx_n, by_n, n_gy),
         out_shape=shaped((levels, nx, ny), f32),
-        in_specs=vmem(4) + [any_hbm] + vmem(1 + n_gy),
-        out_specs=pl.BlockSpec(memory_space=pltpu.VMEM),
+        in_specs=vmem(6 + n_gy),
+        out_specs=any_hbm,
         scratch_shapes=[
             pltpu.VMEM((n_blocks, width), f32),
             pltpu.VMEM((levels, nx, ny), f32),
-            pltpu.SemaphoreType.DMA,
+            pltpu.SemaphoreType.DMA((levels // WARM_BATCH,)),
         ],
         compiler_params=params(),
         name="warm",
-    )(holder, light, flags, tally, in_hbm(stepped), done, *returned)
+    )(holder, light, flags, tally, stepped, done, *returned)
     return thermal_final, out.reshape(solute_amounts.shape)
 
 

time: 64.1 us -> 63.8 us (level)
  no operation moved by 1% of the time
where the time goes in v3:
time: 63.8 us; the launch traced here: 63.6 us
  starting transfers between devices  37.3 us (58%)
  Pallas kernels  22.2 us (35%)
  waiting for transfers between devices  2.57 us (4%)
  between operations  0.83 us (1%)
  local copies, waits for them, and re-layouts  0.64 us (1%)
    ppermute x14, starting transfers between devices, swapped(): return lax.ppermute(x, 'gy', [(i, i ^ d) for i in range(n_gy)])  27 us
    pallas_call x1, Pallas kernels, on_device(): pl.pallas_call(functools.partial(final_kernel, cap), out_shape=[shaped((s...  7.48 us
    all_to_all x1, starting transfers between devices, on_device(): parts = lax.all_to_all(part, ('gx', 'gy'), 0, 0, tiled=True)  5.82 us
    pallas_call x1, Pallas kernels, on_device(): pl.pallas_call(functools.partial(clear_kernel, n_gy), out_shape=[pltpu.VM...  4.54 us
    ppermute x4, starting transfers between devices, traded(): return lax.ppermute(x, axis, pairs + [(j, i) for i, j in pairs])  4.42 us
    pallas_call x1, Pallas kernels, on_device(): pl.pallas_call(functools.partial(warm_kernel, bx_n, by_n, n_gy), out_shap...  3.02 us
    pallas_call x1, Pallas kernels, on_device(): pl.pallas_call(functools.partial(growth_kernel, n_gy), out_shape=[shaped(...  2.42 us
    ppermute x14, waiting for transfers between devices, swapped(): return lax.ppermute(x, 'gy', [(i, i ^ d) for i in range(n_gy)])  2 us
  transfers between devices with their start and end apart: 19, of which 2 were waited for; matrix products, arithmetic and copies ran while one was open for 0% of the time, Pallas kernels for 21%

profile of v3, /device:TPU:0, one launch (start us, length us, event | category | flops | bytes accessed | tf_op | source)
XLA Modules:
  0.0 63.6 jit_solution(7319619012360560890)
XLA Ops:
  0.6 1.4 %edges.1 = (f32[40,128]{1,0:T(8,128)S(1)}, f32[40,128]{1,0:T(8,128)S(1)}, f32[16,128]{1,0:T(8,128)S(1)}, f32[16,128]{1,0:T(8,128)S(1)}, f32[32,32,128]{2,1,0:T(8...) custom-call(f32[32,32,128]{2,1,0:T(8,128)} %refs_0_.1, ...), custom_call_target="tpu_custom_call" | custom-call | tf_op jit(solution)/shard_map/edges/pallas_call | solution.py:520
  2.1 0.6 collective-permute-start
  2.6 0.7 %collective-permute-start.1 = (f32[40,128]{1,0:T(8,128)S(1)}, f32[40,128]{1,0:T(8,128)S(1)}, u32[]{:S(2)}, u32[]{:S(2)}) collective-permute-start(f32[40,128]{1,0:T(8,128)S(1)} %get-tuple-element.45), channel_id=1, source_target_pairs={{8,16},{16,8},{9,17},{17,9},{10,18},{18,10},{11,19},{19,11},{12,20... | collective-permute-start | bytes 61448 | tf_op jit(solution)/shard_map/ppermute | solution.py:536
  3.3 2.6 %collective-permute-start.2 = (f32[16,128]{1,0:T(8,128)S(1)}, f32[16,128]{1,0:T(8,128)S(1)}, u32[]{:S(2)}, u32[]{:S(2)}) collective-permute-start(f32[16,128]{1,0:T(8,128)S(1)} %get-tuple-element.46.own_1), channel_id=1, source_target_pairs={{0,1},{2,3},{4,5},{6,7},{1,0},{3,2},{5,4},{7,6},{8,9},{10,11},{12,... | collective-permute-start | bytes 24584 | tf_op jit(solution)/shard_map/ppermute | solution.py:536
  5.9 0.6 %collective-permute-start.3 = (f32[16,128]{1,0:T(8,128)S(1)}, f32[16,128]{1,0:T(8,128)S(1)}, u32[]{:S(2)}, u32[]{:S(2)}) collective-permute-start(f32[16,128]{1,0:T(8,128)S(1)} %get-tuple-element.47.own_2), channel_id=1, source_target_pairs={{1,2},{3,4},{5,6},{2,1},{4,3},{6,5},{9,10},{11,12},{13,14},{10,9},... | collective-permute-start | bytes 24584 | tf_op jit(solution)/shard_map/ppermute | solution.py:536
  6.5 0.4 slots.1
  6.9 0.6 collective-permute-done.2.y1
  7.5 0.0 collective-permute-done.3.y2
  7.5 0.0 collective-permute-done.x1
  7.5 0.0 collective-permute-done.1.x2
  7.5 1.9 %stencil.1 = (f32[32,32,128]{2,1,0:T(8,128)}, bf16[16,2176]{1,0:T(8,128)(2,1)S(1)}, bf16[16,2176]{1,0:T(8,128)(2,1)S(1)}, bf16[16,2176]{1,0:T(8,128)(2,1)S(1)}, ...) custom-call(f32[32,32,128]{2,1,0:T(8,128)S(1)} %get-tuple-element.43, ...), custom_call_target="tpu_custom_call" | custom-call | tf_op jit(solution)/shard_map/stencil/pallas_call | solution.py:580
  9.5 5.0 %collective-permute-start.4 = (bf16[16,2176]{1,0:T(8,128)(2,1)S(1)}, bf16[16,2176]{1,0:T(8,128)(2,1)S(1)}, u32[]{:S(2)}, u32[]{:S(2)}) collective-permute-start(bf16[16,2176]{1,0:T(8,128)(2,1)S(1)} %get-tuple-element.55), channel_id=1, source_target_pairs={{0,1},{1,0},{2,3},{3,2},{4,5},{5,4},{6,7},{7,6},{8,9},{9,8},{10,11... | collective-permute-start | bytes 208904 | tf_op jit(solution)/shard_map/ppermute | solution.py:594
  14.4 2.0 %collective-permute-start.5 = (bf16[16,2176]{1,0:T(8,128)(2,1)S(1)}, bf16[16,2176]{1,0:T(8,128)(2,1)S(1)}, u32[]{:S(2)}, u32[]{:S(2)}) collective-permute-start(bf16[16,2176]{1,0:T(8,128)(2,1)S(1)} %get-tuple-element.56), channel_id=1, source_target_pairs={{0,2},{1,3},{2,0},{3,1},{4,6},{5,7},{6,4},{7,5},{8,10},{9,11},{10,... | collective-permute-start | bytes 208904 | tf_op jit(solution)/shard_map/ppermute | solution.py:594
  16.4 0.9 %collective-permute-start.6 = (bf16[16,2176]{1,0:T(8,128)(2,1)S(1)}, bf16[16,2176]{1,0:T(8,128)(2,1)S(1)}, u32[]{:S(2)}, u32[]{:S(2)}) collective-permute-start(bf16[16,2176]{1,0:T(8,128)(2,1)S(1)} %get-tuple-element.57), channel_id=1, source_target_pairs={{0,3},{1,2},{2,1},{3,0},{4,7},{5,6},{6,5},{7,4},{8,11},{9,10},{10,... | collective-permute-start | bytes 208904 | tf_op jit(solution)/shard_map/ppermute | solution.py:594
  17.4 3.0 %collective-permute-start.7 = (bf16[16,2176]{1,0:T(8,128)(2,1)S(1)}, bf16[16,2176]{1,0:T(8,128)(2,1)S(1)}, u32[]{:S(2)}, u32[]{:S(2)}) collective-permute-start(bf16[16,2176]{1,0:T(8,128)(2,1)S(1)} %get-tuple-element.58), channel_id=1, source_target_pairs={{0,4},{1,5},{2,6},{3,7},{4,0},{5,1},{6,2},{7,3},{8,12},{9,13},{10,... | collective-permute-start | bytes 208904 | tf_op jit(solution)/shard_map/ppermute | solution.py:594
  20.4 0.0 collective-permute-start.8
  20.4 0.0 collective-permute-done.4.rest_1_
  20.4 3.5 %collective-permute-start.9 = (bf16[16,2176]{1,0:T(8,128)(2,1)S(1)}, bf16[16,2176]{1,0:T(8,128)(2,1)S(1)}, u32[]{:S(2)}, u32[]{:S(2)}) collective-permute-start(bf16[16,2176]{1,0:T(8,128)(2,1)S(1)} %get-tuple-element.60), channel_id=1, source_target_pairs={{0,6},{1,7},{2,4},{3,5},{4,2},{5,3},{6,0},{7,1},{8,14},{9,15},{10,... | collective-permute-start | bytes 208904 | tf_op jit(solution)/shard_map/ppermute | solution.py:594
  23.9 0.0 collective-permute-done.5.rest_2_
  23.9 1.5 %collective-permute-start.10 = (bf16[16,2176]{1,0:T(8,128)(2,1)S(1)}, bf16[16,2176]{1,0:T(8,128)(2,1)S(1)}, u32[]{:S(2)}, u32[]{:S(2)}) collective-permute-start(bf16[16,2176]{1,0:T(8,128)(2,1)S(1)} %get-tuple-element.61), channel_id=1, source_target_pairs={{0,7},{1,6},{2,5},{3,4},{4,3},{5,2},{6,1},{7,0},{8,15},{9,14},{10,... | collective-permute-start | bytes 208904 | tf_op jit(solution)/shard_map/ppermute | solution.py:594
  25.3 4.5 %clear.1 = (f32[128,2048]{1,0:T(8,128)S(1)}, f32[8,16,8,2048]{3,2,1,0:T(8,128)S(1)}, bf16[16,2048]{1,0:T(8,128)(2,1)}, bf16[16,2048]{1,0:T(8,128)(2,1)}, bf16[16...) custom-call(f32[128,8,2048]{2,1,0:T(8,128)} %bitcast.5), custom_call_target="tpu_custom_call" | custom-call | tf_op jit(solution)/shard_map/clear/pallas_call | solution.py:562
  29.9 0.0 copy-start.5
  29.9 0.0 collective-permute-done.6.rest_3_
  29.9 0.0 collective-permute-done.7.rest_4_
  29.9 2.0 %collective-permute-done.8.rest_5_ = bf16[16,2176]{1,0:T(8,128)(2,1)S(1)} collective-permute-done((bf16[16,2176]{1,0:T(8,128)(2,1)S(1)}, bf16[16,2176]{1,0:T(8,128)(2,1)S(1)}, u32[]{:S(2)}, u32[]{:S(2)}) %collective-permute-start.8) | collective-permute-done | bytes 69664 | tf_op jit(solution)/shard_map/ppermute | solution.py:594
  31.9 0.0 collective-permute-done.9.rest_6_
  31.9 0.0 collective-permute-done.10.rest_7_
  31.9 2.4 %growth.1 = (bf16[128,2176]{1,0:T(8,128)(2,1)S(1)}, f32[128,128]{1,0:T(8,128)S(1)}, f32[16,128,128]{2,1,0:T(8,128)S(1)}, f32[32,8,128]{2,1,0:T(8,128)}) custom-call(f32[128,2048]{1,0:T(8,128)S(1)} %get-tuple-element.52.above, f32[8,16,8,2048]{3,2,1,0:T(8,128)S(1)} %get-tuple-element.53.c, bf16[16,2176]{1,0:T(8,128)(2,1)S(1)} %get-tuple-element.54.rest_0_, ...), custom_call_target="tpu_custom_call" | custom-call | tf_op jit(solution)/shard_map/growth/pallas_call | solution.py:600
  34.3 5.8 %all-to-all-start = ((f32[32,8,128]{2,1,0:T(8,128)}), f32[32,8,128]{2,1,0:T(8,128)S(1)}, u32[]{:S(2)}, u32[]{:S(2)}) async-start(f32[32,8,128]{2,1,0:T(8,128)} %get-tuple-element.62), calls=%async_computation | async-start | bytes 262144 | tf_op jit(solution)/shard_map/all_to_all | solution.py:618
  40.1 1.8 %collective-permute-start.11 = (bf16[16,2048]{1,0:T(8,128)(2,1)S(1)}, bf16[16,2048]{1,0:T(8,128)(2,1)S(1)}, u32[]{:S(2)}, u32[]{:S(2)}) collective-permute-start(bf16[16,2048]{1,0:T(8,128)(2,1)S(1)} %copy-done.5), channel_id=1, source_target_pairs={{0,1},{1,0},{2,3},{3,2},{4,5},{5,4},{6,7},{7,6},{8,9},{9,8},{10,11... | collective-permute-start | bytes 196616 | tf_op jit(solution)/shard_map/ppermute | solution.py:594
  42.0 1.5 %collective-permute-start.12 = (bf16[16,2048]{1,0:T(8,128)(2,1)S(1)}, bf16[16,2048]{1,0:T(8,128)(2,1)S(1)}, u32[]{:S(2)}, u32[]{:S(2)}) collective-permute-start(bf16[16,2048]{1,0:T(8,128)(2,1)S(1)} %copy-done.4), channel_id=1, source_target_pairs={{0,2},{1,3},{2,0},{3,1},{4,6},{5,7},{6,4},{7,5},{8,10},{9,11},{10,... | collective-permute-start | bytes 196616 | tf_op jit(solution)/shard_map/ppermute | solution.py:594
  43.4 0.3 collective-permute-start.13
  43.7 2.7 %collective-permute-start.14 = (bf16[16,2048]{1,0:T(8,128)(2,1)}, bf16[16,2048]{1,0:T(8,128)(2,1)}, u32[]{:S(2)}, u32[]{:S(2)}) collective-permute-start(bf16[16,2048]{1,0:T(8,128)(2,1)} %get-tuple-element.71), channel_id=1, source_target_pairs={{0,4},{1,5},{2,6},{3,7},{4,0},{5,1},{6,2},{7,3},{8,12},{9,13},{10,... | collective-permute-start | bytes 196616 | tf_op jit(solution)/shard_map/ppermute | solution.py:594
  46.4 1.5 %collective-permute-start.15 = (bf16[16,2048]{1,0:T(8,128)(2,1)}, bf16[16,2048]{1,0:T(8,128)(2,1)}, u32[]{:S(2)}, u32[]{:S(2)}) collective-permute-start(bf16[16,2048]{1,0:T(8,128)(2,1)} %get-tuple-element.72), channel_id=1, source_target_pairs={{0,5},{1,4},{2,7},{3,6},{4,1},{5,0},{6,3},{7,2},{8,13},{9,12},{10,... | collective-permute-start | bytes 196616 | tf_op jit(solution)/shard_map/ppermute | solution.py:594
  47.8 0.0 collective-permute-done.11.rest_1_
  47.8 3.3 %collective-permute-start.16 = (bf16[16,2048]{1,0:T(8,128)(2,1)}, bf16[16,2048]{1,0:T(8,128)(2,1)}, u32[]{:S(2)}, u32[]{:S(2)}) collective-permute-start(bf16[16,2048]{1,0:T(8,128)(2,1)} %get-tuple-element.73), channel_id=1, source_target_pairs={{0,6},{1,7},{2,4},{3,5},{4,2},{5,3},{6,0},{7,1},{8,14},{9,15},{10,... | collective-permute-start | bytes 196616 | tf_op jit(solution)/shard_map/ppermute | solution.py:594
  51.2 0.0 collective-permute-done.12.rest_2_
  51.2 0.6 copy-done.2
  51.8 0.2 collective-permute-start.17
  52.0 1.0 %mixing.1.mix = f32[16,128,128]{2,1,0:T(8,128)S(1)} custom-call(bf16[128,2176]{1,0:T(8,128)(2,1)S(1)} %get-tuple-element.65.arrived, f32[128,128]{1,0:T(8,128)S(1)} %get-tuple-element.63.counts), custom_call_target="tpu_custom_call" | custom-call | tf_op jit(solution)/shard_map/mixing/pallas_call | solution.py:623
  53.0 0.0 all-to-all-done.parts
  53.0 7.5 %final.1 = (f32[128,8,2048]{2,1,0:T(8,128)}, f32[8,128]{1,0:T(8,128)S(1)}) custom-call(f32[32,8,128]{2,1,0:T(8,128)S(1)} %all-to-all-done.parts, f32[128,128]{1,0:T(8,128)S(1)} %get-tuple-element.63.counts, f32[16,128,128]{2,1,0:T(8,128)S(1)} %get-tuple-element.64.weight, f32[16,128,128]{2,1,0:T(8,128)S(1)} %mixing.1.mix, f32[8,8]{1,0:T(8,128)} %rates_hbm.1, ...), custom_call_target="tpu_custom_call" | custom-call | tf_op jit(solution)/shard_map/final/pallas_call | solution.py:632
  60.5 0.0 collective-permute-done.13.rest_3_
  60.5 0.0 collective-permute-done.14.rest_4_
  60.5 0.0 collective-permute-done.15.rest_5_
  60.5 0.0 collective-permute-done.16.rest_6_
  60.5 0.0 collective-permute-done.17.rest_7_
  60.6 3.0 %warm.1 = f32[32,32,128]{2,1,0:T(8,128)} custom-call(s32[1,64]{1,0:T(1,128)S(1)} %get-tuple-element.39.holder, bf16[32,128]{1,0:T(8,128)(2,1)S(1)} %get-tuple-element.40.light, s32[1,64]{1,0:T(1,128)S(1)} %get-tuple-element.41.flags, s32[1,64]{1,0:T(1,128)S(1)} %get-tuple-element.42.tally, f32[32,32,128]{2,1,0:T(8,128)S(1)} %copy-done, ...), custom_call_target="tpu_custom_call" | custom-call | tf_op jit(solution)/shard_map/warm/pallas_call | solution.py:651
  (10 shorter events, 0.0 us)
Async XLA Ops:
  2.1 5.4 %collective-permute-start = (f32[40,128]{1,0:T(8,128)S(1)}, f32[40,128]{1,0:T(8,128)S(1)}, u32[]{:S(2)}, u32[]{:S(2)}) collective-permute-start(f32[40,128]{1,0:T(8,128)S(1)} %get-tuple-element.44), channel_id=1, source_target_pairs={{0,8},{16,24},{8,0},{24,16},{1,9},{17,25},{9,1},{25,17},{2,10},{18... | collective-permute-start | bytes 61448 | tf_op jit(solution)/shard_map/ppermute | solution.py:536
  2.6 4.9 %collective-permute-start.1 = (f32[40,128]{1,0:T(8,128)S(1)}, f32[40,128]{1,0:T(8,128)S(1)}, u32[]{:S(2)}, u32[]{:S(2)}) collective-permute-start(f32[40,128]{1,0:T(8,128)S(1)} %get-tuple-element.45), channel_id=1, source_target_pairs={{8,16},{16,8},{9,17},{17,9},{10,18},{18,10},{11,19},{19,11},{12,20... | collective-permute-start | bytes 61448 | tf_op jit(solution)/shard_map/ppermute | solution.py:536
  3.3 4.2 %collective-permute-start.2 = (f32[16,128]{1,0:T(8,128)S(1)}, f32[16,128]{1,0:T(8,128)S(1)}, u32[]{:S(2)}, u32[]{:S(2)}) collective-permute-start(f32[16,128]{1,0:T(8,128)S(1)} %get-tuple-element.46.own_1), channel_id=1, source_target_pairs={{0,1},{2,3},{4,5},{6,7},{1,0},{3,2},{5,4},{7,6},{8,9},{10,11},{12,... | collective-permute-start | bytes 24584 | tf_op jit(solution)/shard_map/ppermute | solution.py:536
  5.9 1.6 %collective-permute-start.3 = (f32[16,128]{1,0:T(8,128)S(1)}, f32[16,128]{1,0:T(8,128)S(1)}, u32[]{:S(2)}, u32[]{:S(2)}) collective-permute-start(f32[16,128]{1,0:T(8,128)S(1)} %get-tuple-element.47.own_2), channel_id=1, source_target_pairs={{1,2},{3,4},{5,6},{2,1},{4,3},{6,5},{9,10},{11,12},{13,14},{10,9},... | collective-permute-start | bytes 24584 | tf_op jit(solution)/shard_map/ppermute | solution.py:536
  9.5 10.9 %collective-permute-start.4 = (bf16[16,2176]{1,0:T(8,128)(2,1)S(1)}, bf16[16,2176]{1,0:T(8,128)(2,1)S(1)}, u32[]{:S(2)}, u32[]{:S(2)}) collective-permute-start(bf16[16,2176]{1,0:T(8,128)(2,1)S(1)} %get-tuple-element.55), channel_id=1, source_target_pairs={{0,1},{1,0},{2,3},{3,2},{4,5},{5,4},{6,7},{7,6},{8,9},{9,8},{10,11... | collective-permute-start | bytes 208904 | tf_op jit(solution)/shard_map/ppermute | solution.py:594
  14.4 9.4 %collective-permute-start.5 = (bf16[16,2176]{1,0:T(8,128)(2,1)S(1)}, bf16[16,2176]{1,0:T(8,128)(2,1)S(1)}, u32[]{:S(2)}, u32[]{:S(2)}) collective-permute-start(bf16[16,2176]{1,0:T(8,128)(2,1)S(1)} %get-tuple-element.56), channel_id=1, source_target_pairs={{0,2},{1,3},{2,0},{3,1},{4,6},{5,7},{6,4},{7,5},{8,10},{9,11},{10,... | collective-permute-start | bytes 208904 | tf_op jit(solution)/shard_map/ppermute | solution.py:594
  16.4 13.5 %collective-permute-start.6 = (bf16[16,2176]{1,0:T(8,128)(2,1)S(1)}, bf16[16,2176]{1,0:T(8,128)(2,1)S(1)}, u32[]{:S(2)}, u32[]{:S(2)}) collective-permute-start(bf16[16,2176]{1,0:T(8,128)(2,1)S(1)} %get-tuple-element.57), channel_id=1, source_target_pairs={{0,3},{1,2},{2,1},{3,0},{4,7},{5,6},{6,5},{7,4},{8,11},{9,10},{10,... | collective-permute-start | bytes 208904 | tf_op jit(solution)/shard_map/ppermute | solution.py:594
  17.4 12.5 %collective-permute-start.7 = (bf16[16,2176]{1,0:T(8,128)(2,1)S(1)}, bf16[16,2176]{1,0:T(8,128)(2,1)S(1)}, u32[]{:S(2)}, u32[]{:S(2)}) collective-permute-start(bf16[16,2176]{1,0:T(8,128)(2,1)S(1)} %get-tuple-element.58), channel_id=1, source_target_pairs={{0,4},{1,5},{2,6},{3,7},{4,0},{5,1},{6,2},{7,3},{8,12},{9,13},{10,... | collective-permute-start | bytes 208904 | tf_op jit(solution)/shard_map/ppermute | solution.py:594
  20.4 11.5 %collective-permute-start.8 = (bf16[16,2176]{1,0:T(8,128)(2,1)S(1)}, bf16[16,2176]{1,0:T(8,128)(2,1)S(1)}, u32[]{:S(2)}, u32[]{:S(2)}) collective-permute-start(bf16[16,2176]{1,0:T(8,128)(2,1)S(1)} %get-tuple-element.59), channel_id=1, source_target_pairs={{0,5},{1,4},{2,7},{3,6},{4,1},{5,0},{6,3},{7,2},{8,13},{9,12},{10,... | collective-permute-start | bytes 208904 | tf_op jit(solution)/shard_map/ppermute | solution.py:594
  20.4 11.5 %collective-permute-start.9 = (bf16[16,2176]{1,0:T(8,128)(2,1)S(1)}, bf16[16,2176]{1,0:T(8,128)(2,1)S(1)}, u32[]{:S(2)}, u32[]{:S(2)}) collective-permute-start(bf16[16,2176]{1,0:T(8,128)(2,1)S(1)} %get-tuple-element.60), channel_id=1, source_target_pairs={{0,6},{1,7},{2,4},{3,5},{4,2},{5,3},{6,0},{7,1},{8,14},{9,15},{10,... | collective-permute-start | bytes 208904 | tf_op jit(solution)/shard_map/ppermute | solution.py:594
  23.9 8.0 %collective-permute-start.10 = (bf16[16,2176]{1,0:T(8,128)(2,1)S(1)}, bf16[16,2176]{1,0:T(8,128)(2,1)S(1)}, u32[]{:S(2)}, u32[]{:S(2)}) collective-permute-start(bf16[16,2176]{1,0:T(8,128)(2,1)S(1)} %get-tuple-element.61), channel_id=1, source_target_pairs={{0,7},{1,6},{2,5},{3,4},{4,3},{5,2},{6,1},{7,0},{8,15},{9,14},{10,... | collective-permute-start | bytes 208904 | tf_op jit(solution)/shard_map/ppermute | solution.py:594
  29.9 10.3 %copy-start.5 = (bf16[16,2048]{1,0:T(8,128)(2,1)S(1)}, bf16[16,2048]{1,0:T(8,128)(2,1)}, u32[]{:S(2)}) copy-start(bf16[16,2048]{1,0:T(8,128)(2,1)} %get-tuple-element.68) | copy-start | bytes 196612
  29.9 12.1 %copy-start.4 = (bf16[16,2048]{1,0:T(8,128)(2,1)S(1)}, bf16[16,2048]{1,0:T(8,128)(2,1)}, u32[]{:S(2)}) copy-start(bf16[16,2048]{1,0:T(8,128)(2,1)} %get-tuple-element.69) | copy-start | bytes 196612
  34.3 26.2 %copy-start = (f32[32,32,128]{2,1,0:T(8,128)S(1)}, f32[32,32,128]{2,1,0:T(8,128)}, u32[]{:S(2)}) copy-start(f32[32,32,128]{2,1,0:T(8,128)} %get-tuple-element.51.stepped) | copy-start | bytes 1572868
  34.3 26.2 %copy-start.1 = (bf16[16,2048]{1,0:T(8,128)(2,1)S(1)}, bf16[16,2048]{1,0:T(8,128)(2,1)}, u32[]{:S(2)}) copy-start(bf16[16,2048]{1,0:T(8,128)(2,1)} %get-tuple-element.67.rest_0_) | copy-start | bytes 196612
  34.3 18.7 %all-to-all-start = ((f32[32,8,128]{2,1,0:T(8,128)}), f32[32,8,128]{2,1,0:T(8,128)S(1)}, u32[]{:S(2)}, u32[]{:S(2)}) async-start(f32[32,8,128]{2,1,0:T(8,128)} %get-tuple-element.62), calls=%async_computation | async-start | bytes 262144 | tf_op jit(solution)/shard_map/all_to_all | solution.py:618
  40.1 7.7 %collective-permute-start.11 = (bf16[16,2048]{1,0:T(8,128)(2,1)S(1)}, bf16[16,2048]{1,0:T(8,128)(2,1)S(1)}, u32[]{:S(2)}, u32[]{:S(2)}) collective-permute-start(bf16[16,2048]{1,0:T(8,128)(2,1)S(1)} %copy-done.5), channel_id=1, source_target_pairs={{0,1},{1,0},{2,3},{3,2},{4,5},{5,4},{6,7},{7,6},{8,9},{9,8},{10,11... | collective-permute-start | bytes 196616 | tf_op jit(solution)/shard_map/ppermute | solution.py:594
  42.0 9.2 %collective-permute-start.12 = (bf16[16,2048]{1,0:T(8,128)(2,1)S(1)}, bf16[16,2048]{1,0:T(8,128)(2,1)S(1)}, u32[]{:S(2)}, u32[]{:S(2)}) collective-permute-start(bf16[16,2048]{1,0:T(8,128)(2,1)S(1)} %copy-done.4), channel_id=1, source_target_pairs={{0,2},{1,3},{2,0},{3,1},{4,6},{5,7},{6,4},{7,5},{8,10},{9,11},{10,... | collective-permute-start | bytes 196616 | tf_op jit(solution)/shard_map/ppermute | solution.py:594
  43.4 17.0 %collective-permute-start.13 = (bf16[16,2048]{1,0:T(8,128)(2,1)}, bf16[16,2048]{1,0:T(8,128)(2,1)}, u32[]{:S(2)}, u32[]{:S(2)}) collective-permute-start(bf16[16,2048]{1,0:T(8,128)(2,1)} %get-tuple-element.70), channel_id=1, source_target_pairs={{0,3},{1,2},{2,1},{3,0},{4,7},{5,6},{6,5},{7,4},{8,11},{9,10},{10,... | collective-permute-start | bytes 196616 | tf_op jit(solution)/shard_map/ppermute | solution.py:594
  43.7 16.8 %collective-permute-start.14 = (bf16[16,2048]{1,0:T(8,128)(2,1)}, bf16[16,2048]{1,0:T(8,128)(2,1)}, u32[]{:S(2)}, u32[]{:S(2)}) collective-permute-start(bf16[16,2048]{1,0:T(8,128)(2,1)} %get-tuple-element.71), channel_id=1, source_target_pairs={{0,4},{1,5},{2,6},{3,7},{4,0},{5,1},{6,2},{7,3},{8,12},{9,13},{10,... | collective-permute-start | bytes 196616 | tf_op jit(solution)/shard_map/ppermute | solution.py:594
  46.4 14.1 %collective-permute-start.15 = (bf16[16,2048]{1,0:T(8,128)(2,1)}, bf16[16,2048]{1,0:T(8,128)(2,1)}, u32[]{:S(2)}, u32[]{:S(2)}) collective-permute-start(bf16[16,2048]{1,0:T(8,128)(2,1)} %get-tuple-element.72), channel_id=1, source_target_pairs={{0,5},{1,4},{2,7},{3,6},{4,1},{5,0},{6,3},{7,2},{8,13},{9,12},{10,... | collective-permute-start | bytes 196616 | tf_op jit(solution)/shard_map/ppermute | solution.py:594
  47.8 12.7 %collective-permute-start.16 = (bf16[16,2048]{1,0:T(8,128)(2,1)}, bf16[16,2048]{1,0:T(8,128)(2,1)}, u32[]{:S(2)}, u32[]{:S(2)}) collective-permute-start(bf16[16,2048]{1,0:T(8,128)(2,1)} %get-tuple-element.73), channel_id=1, source_target_pairs={{0,6},{1,7},{2,4},{3,5},{4,2},{5,3},{6,0},{7,1},{8,14},{9,15},{10,... | collective-permute-start | bytes 196616 | tf_op jit(solution)/shard_map/ppermute | solution.py:594
  51.2 0.6 copy-start.2
  51.8 8.7 %collective-permute-start.17 = (bf16[16,2048]{1,0:T(8,128)(2,1)}, bf16[16,2048]{1,0:T(8,128)(2,1)}, u32[]{:S(2)}, u32[]{:S(2)}) collective-permute-start(bf16[16,2048]{1,0:T(8,128)(2,1)} %get-tuple-element.74), channel_id=1, source_target_pairs={{0,7},{1,6},{2,5},{3,4},{4,3},{5,2},{6,1},{7,0},{8,15},{9,14},{10,... | collective-permute-start | bytes 196616 | tf_op jit(solution)/shard_map/ppermute | solution.py:594
  53.0 7.6 %copy-start.3 = (bf16[16,2048]{1,0:T(8,128)(2,1)S(1)}, bf16[16,2048]{1,0:T(8,128)(2,1)}, u32[]{:S(2)}) copy-start(bf16[16,2048]{1,0:T(8,128)(2,1)} %copy-done.2) | copy-start | bytes 196612
